TPU v7x, 32 devices: a whole 2x2x4 slice. The times are simulated.
32 devices in a mesh: rep: 2 (over x), fsdp: 16 (over z, y, core).
Axes of the slice: x: 2, y: 2, z: 4, core: 2. Of those that a mesh axis runs over, the one named last changes fastest.
Arguments:
- x_in: bfloat16 [32, 256, 1536], P(('rep', 'fsdp')), may hold values from -6 to 6
- doc_ids: int32 [32, 256], P(('rep', 'fsdp')), may hold values from 0 to 3, never falling along the last dimension, each value on 1 to 128 neighbouring positions
- w_qkv: bfloat16 [1536, 4608], P('fsdp'), may hold values from -0.15625 to 0.15625
- w_out: bfloat16 [1536, 1536], P('fsdp'), may hold values from -0.15625 to 0.15625
- gain_attn: bfloat16 [1536], P('fsdp'), may hold values from 0.5 to 1.5
- gain_group: bfloat16 [1536], P('fsdp'), may hold values from 0.5 to 1.5
- conv_kernel: float32 [16, 6, 11], replicated, may hold values from -0.8 to 0.8
- head_mix: float32 [16, 2], replicated, may hold values from 0.1 to 1
- gain_ffn: bfloat16 [1536], P('fsdp'), may hold values from 0.5 to 1.5
- w_gate: bfloat16 [1536, 4096], P('fsdp'), may hold values from -0.15625 to 0.15625
- w_up: bfloat16 [1536, 4096], P('fsdp'), may hold values from -0.15625 to 0.15625
- w_down: bfloat16 [4096, 1536], P('fsdp'), may hold values from -0.09375 to 0.09375
- cotangent: bfloat16 [32, 256, 1536], P(('rep', 'fsdp')), may hold values from -6 to 6
Outputs:
- out: bfloat16 [32, 256, 1536], P(('rep', 'fsdp'))
- grad_x: float32 [32, 256, 1536], P(('rep', 'fsdp'))
- grad_qkv: float32 [1536, 4608], P('fsdp')
- grad_out: float32 [1536, 1536], P('fsdp')
- grad_gain_attn: float32 [1536], P('fsdp')
- grad_gain_group: float32 [1536], P('fsdp')
- grad_conv: float32 [16, 6, 11], replicated
- grad_mix: float32 [16, 2], replicated
- grad_gain_ffn: float32 [1536], P('fsdp')
- grad_gate: float32 [1536, 4096], P('fsdp')
- grad_up: float32 [1536, 4096], P('fsdp')
- grad_down: float32 [4096, 1536], P('fsdp')
Inputs may be any that keep to these rules, and one draw needn't show every extreme that they name: `doc_ids`: within each packed row the document ids never fall, and each document holds at most 128 tokens.
All inputs are finite; a program needn't handle non-finite values.
Results may differ from a plain program's by a relative error of at most 0.017.
Values may be sent and summed in bfloat16 or wider, within the bound.
A program may use at most 320 MiB of HBM per device.

v0:
```python
import math

import jax
import jax.numpy as jnp
from jax import lax
from jax.experimental import pallas as pl
from jax.experimental.pallas import tpu as pltpu
from jax.sharding import PartitionSpec as P

MODEL_WIDTH = 1536
H = 16
E = 96
EP = 128
QWIN = 6
KWIN = 11
bf16, f32 = jnp.bfloat16, jnp.float32


def allowed_mask(doc_col, doc_row):
    n = doc_row.shape[-1]
    i = lax.broadcasted_iota(jnp.int32, (n, n), 0)
    j = lax.broadcasted_iota(jnp.int32, (n, n), 1)
    return (j <= i) & (doc_col == doc_row)


def down(v, a):
    if a == 0:
        return v
    i = lax.broadcasted_iota(jnp.int32, v.shape, 0)
    return jnp.where(i >= a, pltpu.roll(v, a, 0), 0.0)


def up(v, a):
    if a == 0:
        return v
    n = v.shape[0]
    i = lax.broadcasted_iota(jnp.int32, v.shape, 0)
    return jnp.where(i < n - a, pltpu.roll(v, n - a, 0), 0.0)


def dot(a, b, ca=1, cb=0):
    return lax.dot_general(a, b, (((ca,), (cb,)), ((), ())), preferred_element_type=f32)


def split(v):
    hi = v.astype(bf16)
    return hi, (v - hi.astype(f32)).astype(bf16)


def attend_row(mix_ref, qkv_ref, dcol_ref, drow_ref, th_ref, tl_ref, gain_ref,
               normed_ref, xhat_ref, s_ref, p_ref, z_ref):
    allowed = allowed_mask(dcol_ref[0], drow_ref[0])
    scale = 1.0 / math.sqrt(E)
    probs = []
    for h in range(2):
        q = qkv_ref[0, :, h * EP:(h + 1) * EP]
        k = qkv_ref[0, :, (2 + h) * EP:(3 + h) * EP]
        zeroed = jnp.where(allowed, dot(q, k, 1, 1) * scale, 0.0)
        z_ref[0, h] = zeroed.astype(bf16)
        his, los = [], []
        for a in range(QWIN):
            hi, lo = split(down(zeroed, a))
            his.append(hi)
            los.append(lo)
        his, los = jnp.concatenate(his, 1), jnp.concatenate(los, 1)
        th, tl = th_ref[h], tl_ref[h]
        conv = dot(his, th) + (dot(his, tl) + dot(los, th))
        masked = jnp.where(allowed, conv, -jnp.inf)
        e = jnp.exp(masked - jnp.max(masked, axis=1, keepdims=True))
        p = e / jnp.sum(e, axis=1, keepdims=True)
        p_ref[0, h] = p
        probs.append(p)
    lane = lax.broadcasted_iota(jnp.int32, (1, EP), 1)
    for h in range(2):
        v = qkv_ref[0, :, (4 + h) * EP:(5 + h) * EP]
        mixed = (mix_ref[h, 0] * probs[0] + mix_ref[h, 1] * probs[1]).astype(bf16)
        ho = dot(mixed, v)
        centered = jnp.where(lane < E, ho - jnp.sum(ho, axis=1, keepdims=True) / E, 0.0)
        s = lax.rsqrt(jnp.sum(centered * centered, axis=1, keepdims=True) / E + 1e-05)
        xhat = centered * s
        cols = slice(h * EP, (h + 1) * EP)
        xhat_ref[0, :, cols] = xhat
        s_ref[0, :, cols] = jnp.broadcast_to(s, xhat.shape)
        normed_ref[0, :, cols] = (xhat * gain_ref[0:1, cols]).astype(bf16)


def attend(mix, qkv, dcol, drow, th, tl, gain):
    n, t, _ = qkv.shape
    row = lambda *s: pl.BlockSpec((1,) + s, lambda i: (i,) + (0,) * len(s))
    full = lambda a: pl.BlockSpec(a.shape, lambda i: (0,) * a.ndim)
    return pl.pallas_call(
        attend_row,
        grid=(n,),
        in_specs=[pl.BlockSpec(memory_space=pltpu.SMEM), row(t, 6 * EP), row(t, 1), row(1, t), full(th), full(tl), full(gain)],
        out_specs=[row(t, 2 * EP), row(t, 2 * EP), row(t, 2 * EP), row(2, t, t), row(2, t, t)],
        out_shape=[
            jax.ShapeDtypeStruct((n, t, 2 * EP), bf16),
            jax.ShapeDtypeStruct((n, t, 2 * EP), f32),
            jax.ShapeDtypeStruct((n, t, 2 * EP), f32),
            jax.ShapeDtypeStruct((n, 2, t, t), f32),
            jax.ShapeDtypeStruct((n, 2, t, t), bf16),
        ],
        cost_estimate=pl.CostEstimate(flops=n * 2 * 3 * 2 * t * t * QWIN * t, bytes_accessed=n * t * t * 20, transcendentals=n * 2 * t * t),
        name="attend",
    )(mix, qkv, dcol, drow, th, tl, gain)


def bwd_kernel(mix_ref, qkv_ref, dcol_ref, drow_ref, tt_ref, gain_ref, dn_ref, xhat_ref, s_ref, p_ref, z_ref,
               dqkv_ref, gconv_ref, gmix_ref, gg_ref, m_ref):
    step, steps = pl.program_id(0), pl.num_programs(0)
    t = p_ref.shape[-1]

    @pl.when(step == 0)
    def _():
        m_ref[...] = jnp.zeros_like(m_ref)
        gmix_ref[...] = jnp.zeros_like(gmix_ref)
        gg_ref[...] = jnp.zeros_like(gg_ref)

    allowed = allowed_mask(dcol_ref[0], drow_ref[0])
    scale = 1.0 / math.sqrt(E)
    lane = lax.broadcasted_iota(jnp.int32, (1, EP), 1)
    p = [p_ref[0, 0], p_ref[0, 1]]
    dmixed = []
    for h in range(2):
        cols = slice(h * EP, (h + 1) * EP)
        dn, xhat = dn_ref[0, :, cols], xhat_ref[0, :, cols]
        gg_ref[0:1, cols] += jnp.sum(dn * xhat, axis=0, keepdims=True)
        dc = dn * gain_ref[0:1, cols]
        m1 = jnp.sum(dc, axis=1, keepdims=True) / E
        m2 = jnp.sum(dc * xhat, axis=1, keepdims=True) / E
        dh = jnp.where(lane < E, s_ref[0, :, cols] * (dc - m1 - xhat * m2), 0.0).astype(bf16)
        v = qkv_ref[0, :, (4 + h) * EP:(5 + h) * EP]
        mixed = (mix_ref[h, 0] * p[0] + mix_ref[h, 1] * p[1]).astype(bf16)
        dmixed.append(dot(dh, v, 1, 1))
        dqkv_ref[0, :, (4 + h) * EP:(5 + h) * EP] = dot(mixed, dh, 0, 0).astype(bf16)
    for h in range(2):
        for c in range(2):
            r = 2 * h + c
            gmix_ref[r:r + 1, :] += jnp.sum(dmixed[h] * p[c], axis=0, keepdims=True)
    for c in range(2):
        dp = mix_ref[0, c] * dmixed[0] + mix_ref[1, c] * dmixed[1]
        dconv = p[c] * (dp - jnp.sum(dp * p[c], axis=1, keepdims=True))
        ahead = jnp.concatenate([up(dconv, a).astype(bf16) for a in range(QWIN)], 1)
        m_ref[c] += dot(z_ref[0, c], ahead, 0, 0)
        ds = jnp.where(allowed, dot(ahead, tt_ref[c]), 0.0).astype(bf16)
        q = qkv_ref[0, :, c * EP:(c + 1) * EP]
        k = qkv_ref[0, :, (2 + c) * EP:(3 + c) * EP]
        dqkv_ref[0, :, c * EP:(c + 1) * EP] = (dot(ds, k) * scale).astype(bf16)
        dqkv_ref[0, :, (2 + c) * EP:(3 + c) * EP] = (dot(ds, q, 0, 0) * scale).astype(bf16)

    @pl.when(step == steps - 1)
    def _():
        lanes = lax.broadcasted_iota(jnp.int32, (8, t), 1)
        for h in range(2):
            for a in range(QWIN):
                total = jnp.zeros((8, t), f32)
                for first in range(0, t, 8):
                    rows = m_ref[h, first:first + 8, a * t:(a + 1) * t]
                    turned = pltpu.roll(rows, t - first, 1) if first else rows
                    total = total + jnp.where(lanes < t - first, turned, 0.0)
                gconv_ref[h, a] = total[:, :EP]


def attend_back(mix, qkv, dcol, drow, tt, gain, dn, xhat, s, p, z):
    n, t, _ = qkv.shape
    row = lambda *sh: pl.BlockSpec((1,) + sh, lambda i: (i,) + (0,) * len(sh))
    full = lambda a: pl.BlockSpec(a.shape, lambda i: (0,) * a.ndim)
    keep = lambda *sh: pl.BlockSpec(sh, lambda i: (0,) * len(sh))
    return pl.pallas_call(
        bwd_kernel,
        grid=(n,),
        in_specs=[pl.BlockSpec(memory_space=pltpu.SMEM), row(t, 6 * EP), row(t, 1), row(1, t), full(tt), full(gain),
                  row(t, 2 * EP), row(t, 2 * EP), row(t, 2 * EP), row(2, t, t), row(2, t, t)],
        out_specs=[row(t, 6 * EP), keep(2, QWIN, 8, EP), keep(8, t), keep(8, 2 * EP)],
        out_shape=[
            jax.ShapeDtypeStruct((n, t, 6 * EP), bf16),
            jax.ShapeDtypeStruct((2, QWIN, 8, EP), f32),
            jax.ShapeDtypeStruct((8, t), f32),
            jax.ShapeDtypeStruct((8, 2 * EP), f32),
        ],
        scratch_shapes=[pltpu.VMEM((2, t, QWIN * t), f32)],
        cost_estimate=pl.CostEstimate(flops=n * 2 * 2 * 2 * t * t * QWIN * t, bytes_accessed=n * t * t * 20, transcendentals=0),
        name="attend_back",
    )(mix, qkv, dcol, drow, tt, gain, dn, xhat, s, p, z)


def bands(kernel, t):
    diff = jnp.arange(t)[None, :] - jnp.arange(t)[:, None]
    band = jnp.zeros((2, QWIN, t, t), f32)
    back = jnp.zeros((2, QWIN, t, t), f32)
    for b in range(KWIN):
        tap = kernel[:, :, b][:, :, None, None]
        band = band + jnp.where(diff == b, tap, 0.0)
        back = back + jnp.where(diff == -b, tap, 0.0)
    th, tl = split(band)
    flat = lambda v: v.reshape(2, QWIN * t, t)
    return flat(th), flat(tl), flat(back.astype(bf16))


def diagonals(tiles):
    return sum(tiles[:, :, i, i:i + KWIN] for i in range(8))


FF = 4096
MESH = pl.DeviceIdType.MESH


class Net:
    def __init__(self):
        self.x, self.f = lax.axis_index("rep"), lax.axis_index("fsdp")
        self.z, self.y, self.c = self.f // 4, (self.f // 2) % 2, self.f % 2
        self.k = self.f % 4
        nx, fy, fc = 1 - self.x, 2 - 4 * self.y, 1 - 2 * self.c
        self.to = {
            "x": (nx, self.f),
            "y": (self.x, self.f + fy),
            "c": (self.x, self.f + fc),
            "xy": (nx, self.f + fy),
            "xc": (nx, self.f + fc),
            "yc": (self.x, self.f + fy + fc),
            "xyc": (nx, self.f + fy + fc),
            "up": (self.x, self.f + 4),
            "down": (self.x, self.f - 4),
        }

    def greet(self, names, line=True):
        barrier = pltpu.get_barrier_semaphore()
        for name in names:
            pl.semaphore_signal(barrier, inc=1, device_id=self.to[name], device_id_type=MESH)
        count = len(names)
        if line:

            @pl.when(self.z < 3)
            def _():
                pl.semaphore_signal(barrier, inc=1, device_id=self.to["up"], device_id_type=MESH)

            @pl.when(self.z > 0)
            def _():
                pl.semaphore_signal(barrier, inc=1, device_id=self.to["down"], device_id_type=MESH)

            count = count + (self.z + 3) // 4 + (6 - self.z) // 4
        pl.semaphore_wait(barrier, count)

    def copy(self, src, dst, sems, i, name):
        return pltpu.make_async_remote_copy(
            src_ref=src, dst_ref=dst, send_sem=sems[0].at[i], recv_sem=sems[1].at[i],
            device_id=self.to[name], device_id_type=MESH,
        )

    def send(self, src, dst, sems, i, name):
        copy = self.copy(src, dst, sems, i, name)
        copy.start()
        return copy


def tiles(start, size, body, step=32):
    def one(i, _):
        body(pl.ds(pl.multiple_of(start + i * step, step), step))
        return 0

    lax.fori_loop(0, size // step, one, 0)


def wide(v):
    return v.astype(f32)


class GatherLine:
    def __init__(self, net, src, out, sems, base, keep=None):
        self.net, self.src, self.out, self.sems, self.base = net, src, out, sems, base
        self.keep = keep or (lambda slot: net.z >= 0)

    def go(self, d, way, act):
        net = self.net
        slot = net.z - d if way == "up" else net.z + d
        inside = (net.z >= d) & (net.z < 3) if way == "up" else (net.z < 4 - d) & (net.z > 0)
        i = self.base + d + (0 if way == "up" else 3)

        @pl.when(inside & self.keep(slot))
        def _():
            src = self.src if d == 0 else self.out.at[slot]
            act(net.copy(src, self.out.at[slot], self.sems, i, way))

    def came(self, d, way):
        net = self.net
        slot = net.z - d if way == "up" else net.z + d
        inside = net.z >= d if way == "up" else net.z < 4 - d
        i = self.base + d - 1 + (0 if way == "up" else 3)

        @pl.when(inside & self.keep(slot))
        def _():
            net.copy(self.out.at[slot], self.out.at[slot], self.sems, i, way).wait_recv()

    def step(self, d):
        for way in ("up", "down"):
            if d > 0:
                self.came(d, way)
            if d < 3:
                self.go(d, way, lambda copy: copy.start())

    def finish(self):
        for d in range(3):
            for way in ("up", "down"):
                self.go(d, way, lambda copy: copy.wait_send())


class ScatterLine:
    def __init__(self, net, parts, got, made, sems, base):
        self.net, self.parts, self.got, self.made, self.sems, self.base = net, parts, got, made, sems, base
        self.n = parts.shape[1]

    def each(self, d, way):
        net = self.net
        t = net.z + (3 - d) if way == 0 else net.z - (3 - d)
        inside = (t < 4) if way == 0 else (t >= 0)
        first = (net.z == 0) if way == 0 else (net.z == 3)
        return t, inside, first, self.base + d + 3 * way, ("up", "down")[way]

    def step(self, d):
        for way in range(2):
            t, inside, first, i, name = self.each(d, way)

            @pl.when(inside & first)
            def _():
                self.net.copy(self.parts.at[t], self.got.at[way, d], self.sems, i, name).start()

            if d == 0:
                continue

            @pl.when(inside & jnp.logical_not(first))
            def _():
                self.net.copy(self.got.at[way, d - 1], self.got.at[way, d - 1], self.sems, i - 1, name).wait_recv()

                def body(rows):
                    self.made[way, d - 1, rows] = (wide(self.parts[t, rows]) + wide(self.got[way, d - 1, rows])).astype(bf16)

                tiles(0, self.n, body)
                self.net.copy(self.made.at[way, d - 1], self.got.at[way, d], self.sems, i, name).start()

    def finish(self, store):
        net = self.net
        below, above = net.z > 0, net.z < 3

        @pl.when(below)
        def _():
            net.copy(self.got.at[0, 2], self.got.at[0, 2], self.sems, self.base + 2, "up").wait_recv()

        @pl.when(above)
        def _():
            net.copy(self.got.at[1, 2], self.got.at[1, 2], self.sems, self.base + 5, "down").wait_recv()

        def put(low, high):
            def body(rows):
                total = wide(self.parts[net.z, rows])
                if low:
                    total = total + wide(self.got[0, 2, rows])
                if high:
                    total = total + wide(self.got[1, 2, rows])
                store(rows, total)

            tiles(0, self.n, body)

        @pl.when(below & above)
        def _():
            put(True, True)

        @pl.when(jnp.logical_not(below))
        def _():
            put(False, True)

        @pl.when(jnp.logical_not(above))
        def _():
            put(True, False)

        for d in range(3):
            for way in range(2):
                t, inside, first, i, name = self.each(d, way)

                @pl.when(inside & first)
                def _():
                    net.copy(self.parts.at[t], self.got.at[way, d], self.sems, i, name).wait_send()

                if d > 0:

                    @pl.when(inside & jnp.logical_not(first))
                    def _():
                        net.copy(self.made.at[way, d - 1], self.got.at[way, d], self.sems, i, name).wait_send()


def line_scratch(n, w):
    return [pltpu.VMEM((2, 3, n, w), bf16), pltpu.VMEM((2, 2, n, w), bf16)]


LINE_COPIES = 6


class Later:
    def __init__(self, make):
        self.make = make
        make().start()

    def wait_recv(self):
        self.make().wait_recv()

    def wait_send(self):
        self.make().wait_send()


def gather_steps(net, v, out, sems, base, ready):
    n = v.shape[0]
    A, B = pl.ds(0, n // 2), pl.ds(n // 2, n // 2)
    go = {}
    ready(0)
    go["xA"] = Later(lambda: net.copy(v.at[A], out.at[1, 0, A], sems, base + 0, "x"))
    go["yA"] = Later(lambda: net.copy(v.at[A], out.at[2, 0, A], sems, base + 3, "y"))
    go["0A"] = Later(lambda: net.copy(v.at[A], out.at[0, 1, A], sems, base + 4, "c"))
    ready(1)
    go["yB"] = Later(lambda: net.copy(v.at[B], out.at[2, 0, B], sems, base + 2, "y"))
    go["xB"] = Later(lambda: net.copy(v.at[B], out.at[1, 0, B], sems, base + 1, "x"))
    go["0B"] = Later(lambda: net.copy(v.at[B], out.at[0, 1, B], sems, base + 5, "c"))
    yield
    go["xA"].wait_recv()
    go["dA"] = Later(lambda: net.copy(out.at[1, 0, A], out.at[3, 0, A], sems, base + 6, "y"))
    go["1A"] = Later(lambda: net.copy(out.at[1, 0, A], out.at[1, 1, A], sems, base + 8, "c"))
    go["yA"].wait_recv()
    go["2A"] = Later(lambda: net.copy(out.at[2, 0, A], out.at[2, 1, A], sems, base + 10, "c"))
    yield
    go["yB"].wait_recv()
    go["dB"] = Later(lambda: net.copy(out.at[2, 0, B], out.at[3, 0, B], sems, base + 7, "x"))
    go["2B"] = Later(lambda: net.copy(out.at[2, 0, B], out.at[2, 1, B], sems, base + 9, "c"))
    go["xB"].wait_recv()
    go["1B"] = Later(lambda: net.copy(out.at[1, 0, B], out.at[1, 1, B], sems, base + 11, "c"))
    yield
    go["dA"].wait_recv()
    go["3A"] = Later(lambda: net.copy(out.at[3, 0, A], out.at[3, 1, A], sems, base + 12, "c"))
    go["dB"].wait_recv()
    go["3B"] = Later(lambda: net.copy(out.at[3, 0, B], out.at[3, 1, B], sems, base + 13, "c"))
    yield
    for name in ("0A", "0B", "1A", "2B", "2A", "1B", "3A", "3B"):
        go[name].wait_recv()
    for copy in go.values():
        copy.wait_send()


def gather_rows(net, v, out, sems, base, ready, poll):
    for _ in gather_steps(net, v, out, sems, base, ready):
        poll()


GATHER_COPIES = 14
SCATTER_COPIES = 10


def scatter_steps(net, parts, rc, rd, rx, ry, td, tx, ty, sems, base):
    n = parts.shape[2]
    A, B = pl.ds(0, n // 2), pl.ds(n // 2, n // 2)
    go = {}
    for i, chip in enumerate((3, 1, 2, 0)):
        go[chip] = Later(lambda i=i, chip=chip: net.copy(parts.at[chip, 1], rc.at[chip], sems, base + i, "c"))

    def add(dst, chip, start, more=None):
        def body(rows):
            total = wide(parts[chip, 0, rows]) + wide(rc[chip, rows])
            if more is not None:
                total = total + wide(more[rows])
            dst[rows] = total.astype(bf16)

        tiles(start, n // 2, body)

    yield None
    go[3].wait_recv()
    add(td, 3, 0)
    go["dA"] = Later(lambda: net.copy(td.at[A], rd.at[A], sems, base + 4, "x"))
    add(td, 3, n // 2)
    go["dB"] = Later(lambda: net.copy(td.at[B], rd.at[B], sems, base + 5, "y"))
    go[1].wait_recv()
    add(tx, 1, 0)
    go["xA"] = Later(lambda: net.copy(tx.at[A], rx.at[A], sems, base + 6, "x"))
    go[2].wait_recv()
    add(ty, 2, n // 2)
    go["yB"] = Later(lambda: net.copy(ty.at[B], ry.at[B], sems, base + 7, "y"))
    yield None
    go["dA"].wait_recv()
    add(ty, 2, 0, rd)
    go["yA"] = Later(lambda: net.copy(ty.at[A], ry.at[A], sems, base + 8, "y"))
    go["dB"].wait_recv()
    add(tx, 1, n // 2, rd)
    go["xB"] = Later(lambda: net.copy(tx.at[B], rx.at[B], sems, base + 9, "x"))
    go[0].wait_recv()

    def done(half):
        for name in (("xA", "yA"), ("xB", "yB"))[half]:
            go[name].wait_recv()
        if half == 1:
            for copy in go.values():
                copy.wait_send()

    yield done


def scatter_rows(net, parts, rc, rd, rx, ry, td, tx, ty, sems, base, poll):
    steps = scatter_steps(net, parts, rc, rd, rx, ry, td, tx, ty, sems, base)
    next(steps)
    next(steps)
    poll()
    return next(steps)


def scatter_scratch(n, w):
    return [pltpu.VMEM((4, n, w), bf16)] + [pltpu.VMEM((n, w), bf16)] * 6


def dma_sems(count):
    return [pltpu.SemaphoreType.DMA((count,)), pltpu.SemaphoreType.DMA((count,))]


VM = pl.BlockSpec(memory_space=pltpu.VMEM)
ANY = pl.BlockSpec(memory_space=pl.ANY)


def polls(*acts):
    left = list(acts)

    def poll():
        if left:
            left.pop(0)()

    def drain():
        while left:
            poll()

    return poll, drain


def comm_call(body, name, ident, ins, in_specs, outs, out_specs, scratch):
    return pl.pallas_call(
        body,
        in_specs=in_specs,
        out_specs=out_specs,
        out_shape=outs,
        scratch_shapes=scratch,
        compiler_params=pltpu.CompilerParams(collective_id=ident, has_side_effects=True, vmem_limit_bytes=63 << 20),
        name=name,
    )(*ins)


def shape(dims, dtype):
    return jax.ShapeDtypeStruct(dims, dtype)


PLANE = ("x", "y", "c", "xy", "xc", "yc", "xyc")
PLACES = {"c": (0, 1), "x": (1, 0), "xc": (1, 1), "y": (2, 0), "yc": (2, 1), "xy": (3, 0), "xyc": (3, 1)}


def start_call(x, dy, docs, gains, taps, w_qkv, w_gate, w_up, w_out, ident):
    n, w = x.shape
    rows = w_qkv.shape[0]

    def body(x_ref, dy_ref, docs_ref, g_ref, taps_ref, wq_ref, gate_ref, up_ref, wo_ref,
             a1_ref, dys_ref, docs_out, gains_ref, qkv_out, gu_out, wo_out, th_ref, tl_ref, tt_ref,
             xs, gains_out, slots, gus, local, send, recv):
        net = Net()
        sems = (send, recv)
        base = 2 * GATHER_COPIES
        mine = dy_ref.at[pl.ds(0, n // 2)]
        line_q = GatherLine(net, qkv_out.at[net.z], qkv_out, sems, base)
        line_o = GatherLine(net, wo_ref, wo_out, sems, base + 6, lambda slot: slot // 2 == net.x)
        line_g = GatherLine(net, gains_out.at[net.z], gains_out, sems, base + 12)
        base += 18
        gains_out[net.z, net.k] = g_ref[...]
        slots[...] = jnp.zeros_like(slots)
        for half in range(2):

            @pl.when(net.x == half)
            def _():
                for k in range(4):
                    pair = 4 * half + 2 * (k % 2) + k // 2
                    for m in range(6):
                        col = (m // 2) * MODEL_WIDTH + (2 * pair + m % 2) * E
                        slots[k, :, m * EP : m * EP + E] = wq_ref[:, col : col + E]
                    for m in range(8):
                        src = gate_ref if m < 4 else up_ref
                        col = 256 * (4 * (m % 4) + k) + 128 * half
                        gus[k, :, m * 128 : (m + 1) * 128] = src[:, col : col + 128]

        net.greet(PLANE)
        own = [
            pltpu.make_async_copy(mine, dys_ref.at[0, 0], local.at[1]),
            pltpu.make_async_copy(slots.at[net.k], qkv_out.at[net.z, net.k], local.at[0]),
            pltpu.make_async_copy(gus.at[net.k], gu_out.at[net.k], local.at[2]),
            pltpu.make_async_copy(docs_ref, docs_out.at[0, 0], local.at[3]),
            pltpu.make_async_copy(wo_ref, wo_out.at[net.z], local.at[4]),
        ]
        for copy in own:
            copy.start()
        qkv_parts, gain_parts, small = [], [], []
        flips = {"c": net.k + 1 - 2 * net.c, "y": net.k + 2 - 4 * net.y, "yc": net.k + 1 - 2 * net.c + 2 - 4 * net.y}
        for j, name in enumerate(("y", "yc", "c")):
            gain_parts.append(net.send(g_ref, gains_out.at[net.z, net.k], sems, base + 6 + j, name))
            qkv_parts.append(net.send(slots.at[flips[name]], qkv_out.at[net.z, net.k], sems, base + j, name))
        line_o.step(0)
        for j, (name, (chip, core)) in enumerate(PLACES.items()):
            small.append(net.send(docs_ref, docs_out.at[chip, core], sems, base + 9 + j, name))
        gather_x = gather_steps(net, x_ref, xs, sems, 0, lambda half: None)
        next(gather_x)
        gather_dy = gather_steps(net, mine, dys_ref, sems, GATHER_COPIES, lambda half: None)
        next(gather_dy)
        for copy in gain_parts:
            copy.wait_recv()
        line_g.step(0)
        own[1].wait()
        for copy in qkv_parts:
            copy.wait_recv()
        line_q.step(0)
        line_g.step(1)

        diff = lax.broadcasted_iota(jnp.int32, (n, n), 1) - lax.broadcasted_iota(jnp.int32, (n, n), 0)

        def bands_of(first, count):
            def one(i, _):
                band = jnp.zeros((n, n), f32)
                back = jnp.zeros((n, n), f32)
                for b in range(KWIN):
                    tap = taps_ref[(first + i) * KWIN + b]
                    band = jnp.where(diff == b, tap, band)
                    back = jnp.where(diff == -b, tap, back)
                h, a = (first + i) // QWIN, (first + i) % QWIN
                at = pl.ds(pl.multiple_of(a * n, n), n)
                th_ref[h, at], tl_ref[h, at] = split(band)
                tt_ref[h, at] = back.astype(bf16)
                return 0

            lax.fori_loop(0, count, one, 0)

        bands_of(0, QWIN)
        line_g.step(2)
        next(gather_x)
        line_q.step(1)
        line_g.step(3)
        line_o.step(1)
        for i in range(16):
            gains_ref[:, i * rows : (i + 1) * rows] = wide(gains_out[i // 4, i % 4, 0:8, 0:rows])
        bands_of(QWIN, QWIN)
        next(gather_x)
        for j, name in enumerate(("y", "yc", "c")):
            small.append(net.send(gus.at[flips[name]], gu_out.at[net.k], sems, base + 3 + j, name))
        gain = gains_ref[0:1]

        def norm(chip, core, src):
            def body(at):
                xf = wide(src[at])
                r = lax.rsqrt(jnp.mean(xf * xf, axis=1, keepdims=True) + 1e-06)
                a1_ref[chip, core, at] = (xf * r * gain).astype(bf16)

            tiles(0, n, body)

        norm(0, 0, x_ref)
        line_q.step(2)
        line_o.step(2)
        for _ in gather_x:
            pass
        next(gather_dy)
        next(gather_dy)
        for chip in range(4):
            for core in range(2):
                if (chip, core) != (0, 0):
                    norm(chip, core, xs.at[chip, core])
        next(gather_dy)
        line_q.step(3)
        for _ in gather_dy:
            pass
        line_o.step(3)
        for line in (line_q, line_g, line_o):
            line.finish()
        for copy in own[:1] + own[2:]:
            copy.wait()
        for copy in small:
            copy.wait_recv()
        for copy in qkv_parts + gain_parts + small:
            copy.wait_send()

    return comm_call(
        body, "start", ident, (x, dy, docs, gains, taps, w_qkv, w_gate, w_up, w_out),
        [VM] * 4 + [pl.BlockSpec(memory_space=pltpu.SMEM)] + [VM] * 4,
        [shape((4, 2, n, w), bf16), shape((4, 2, n // 2, w), bf16), shape((4, 2) + docs.shape, docs.dtype), shape((8, w), f32),
         shape((4, 4, rows, 6 * EP), bf16), shape((4, rows, FF // 4), bf16), shape((4, rows, MODEL_WIDTH), bf16)]
        + [shape((2, QWIN * n, n), bf16)] * 3,
        [VM, ANY, ANY, VM, ANY, ANY, ANY, VM, VM, VM],
        [pltpu.VMEM((4, 2, n, w), bf16), pltpu.VMEM((4, 4) + gains.shape, bf16),
         pltpu.VMEM((4, rows, 6 * EP), bf16), pltpu.VMEM((4, rows, FF // 4), bf16), pltpu.SemaphoreType.DMA((5,))]
        + dma_sems(2 * GATHER_COPIES + 18 + 16),
    )


def forward_call(mix, a1, dcol, drow, th, tl, group, qkv_w, out_w, x, dy, gain, gu, w_down, ident):
    rows, t, w = a1.shape
    n = x.shape[0]
    down = w_down.shape[0] // 2

    def body(mix_ref, a1_ref, dcol_ref, drow_ref, th_ref, tl_ref, group_ref, qw_ref, ow_ref, x_ref, dy_ref, g_ref, gu_ref, wd_ref,
             qkv_ref, normed_ref, xhat_ref, s_ref, p_ref, z_ref, resid_ref, out_ref, dys_ref, gu_out, wd_out,
             parts, v, local, rc, rd, rx, ry, td, tx, ty, send, recv):
        net = Net()
        sems = (send, recv)
        step = pl.program_id(0)
        base = SCATTER_COPIES + GATHER_COPIES
        mine = wd_ref.at[pl.ds(pl.multiple_of(down * net.x, down), down)]
        line_g = GatherLine(net, gu_ref, gu_out, sems, base)
        line_d = GatherLine(net, mine, wd_out, sems, base + LINE_COPIES)
        own_g = lambda: pltpu.make_async_copy(gu_ref, gu_out.at[net.z], local.at[1])
        own_d = lambda: pltpu.make_async_copy(mine, wd_out.at[net.z], local.at[2])
        A, B = pl.ds(0, n // 2), pl.ds(n // 2, n // 2)
        go = {}
        half_dy = dy_ref.at[pl.ds(n // 2, n // 2)]
        own_dy = lambda: pltpu.make_async_copy(half_dy, dys_ref.at[0, 0], local.at[3])
        gather_dy = gather_steps(net, half_dy, dys_ref, sems, base + 2 * LINE_COPIES, lambda half: None)

        def at(i):
            def run(act):
                pl.when(step == i)(act)

            return run

        @at(0)
        def _():
            net.greet("xyc")
            line_g.step(0)
            line_d.step(0)
            own_g().start()
            own_d().start()
            own_dy().start()
            next(gather_dy)

        qkv_ref[0] = dot(a1_ref[0], qw_ref[...]).astype(bf16)
        attend_row(mix_ref, qkv_ref, dcol_ref, drow_ref, th_ref, tl_ref, group_ref, normed_ref, xhat_ref, s_ref, p_ref, z_ref)
        parts[3 - step // 2, step % 2] = dot(normed_ref[0], ow_ref[...]).astype(bf16)

        def swap(chip, i):
            go[chip] = Later(lambda: net.copy(parts.at[chip, 1], rc.at[chip], sems, i, "c"))

        def add(dst, chip, start, more=None):
            def one(r):
                total = wide(parts[chip, 0, r]) + wide(rc[chip, r])
                if more is not None:
                    total = total + wide(more[r])
                dst[r] = total.astype(bf16)

            tiles(start, n // 2, one)

        @at(1)
        def _():
            swap(3, 0)

        @at(2)
        def _():
            go[3].wait_recv()
            add(td, 3, 0)
            go["dA"] = Later(lambda: net.copy(td.at[A], rd.at[A], sems, 4, "x"))
            add(td, 3, n // 2)
            go["dB"] = Later(lambda: net.copy(td.at[B], rd.at[B], sems, 5, "y"))

        @at(3)
        def _():
            swap(2, 2)
            line_g.step(1)
            next(gather_dy)

        @at(4)
        def _():
            go[2].wait_recv()
            add(ty, 2, n // 2)
            go["yB"] = Later(lambda: net.copy(ty.at[B], ry.at[B], sems, 7, "y"))
            go["dA"].wait_recv()
            add(ty, 2, 0, rd)
            go["yA"] = Later(lambda: net.copy(ty.at[A], ry.at[A], sems, 8, "y"))
            next(gather_dy)

        @at(5)
        def _():
            swap(1, 1)
            line_d.step(1)
            next(gather_dy)

        @at(6)
        def _():
            go[1].wait_recv()
            add(tx, 1, 0)
            go["xA"] = Later(lambda: net.copy(tx.at[A], rx.at[A], sems, 6, "x"))
            go["dB"].wait_recv()
            add(tx, 1, n // 2, rd)
            go["xB"] = Later(lambda: net.copy(tx.at[B], rx.at[B], sems, 9, "x"))

        @at(rows - 1)
        def _():
            swap(0, 3)
            line_g.step(2)
            for _ in gather_dy:
                pass
            go[0].wait_recv()

            def ready(half):
                for name in (("yA", "xA"), ("yB", "xB"))[half]:
                    go[name].wait_recv()

                def rows_of(r):
                    total = wide(parts[0, 0, r]) + wide(rc[0, r]) + wide(rx[r]) + wide(ry[r])
                    resid = wide(x_ref[r]) + total
                    resid_ref[r] = resid
                    inv = lax.rsqrt(jnp.mean(resid * resid, axis=1, keepdims=True) + 1e-06)
                    v[r] = (resid * inv * g_ref[...]).astype(bf16)

                tiles(half * (n // 2), n // 2, rows_of)

            poll, drain = polls(lambda: line_d.step(2), lambda: line_g.step(3), lambda: line_d.step(3))
            gather_rows(net, v, out_ref, sems, SCATTER_COPIES, ready, poll)
            drain()
            last = pltpu.make_async_copy(v, out_ref.at[0, 0], local.at[0])
            last.start()
            line_g.finish()
            line_d.finish()
            own_g().wait()
            own_d().wait()
            own_dy().wait()
            for copy in go.values():
                copy.wait_send()
            last.wait()

    where = lambda i: 2 * (3 - i // 2) + i % 2
    row = lambda *sh: pl.BlockSpec((1,) + sh, lambda i: (where(i),) + (0,) * len(sh))
    full = lambda v: pl.BlockSpec(v.shape, lambda i: (0,) * v.ndim, pipeline_mode=pl.Buffered(1))
    keep = lambda *sh: pl.BlockSpec(sh, lambda i: (0,) * len(sh))
    return pl.pallas_call(
        body,
        grid=(rows,),
        in_specs=[pl.BlockSpec(memory_space=pltpu.SMEM), row(t, w), row(t, 1), row(1, t), full(th), full(tl), full(group), full(qkv_w),
                  full(out_w), full(x), full(dy), full(gain), full(gu), full(w_down)],
        out_specs=[row(t, 6 * EP), row(t, 2 * EP), row(t, 2 * EP), row(t, 2 * EP), row(2, t, t), row(2, t, t), keep(n, w), ANY, ANY, ANY, ANY],
        out_shape=[
            shape((rows, t, 6 * EP), bf16),
            shape((rows, t, 2 * EP), bf16),
            shape((rows, t, 2 * EP), f32),
            shape((rows, t, 2 * EP), f32),
            shape((rows, 2, t, t), f32),
            shape((rows, 2, t, t), bf16),
            shape((n, w), f32),
            shape((4, 2, n, w), bf16),
            shape((4, 2, n // 2, w), bf16),
            shape((4,) + gu.shape, bf16),
            shape((4, down, w), bf16),
        ],
        scratch_shapes=[pltpu.VMEM((4, 2, n, w), bf16), pltpu.VMEM((n, w), bf16), pltpu.SemaphoreType.DMA((4,))] + scatter_scratch(n, w)
        + dma_sems(SCATTER_COPIES + 2 * GATHER_COPIES + 2 * LINE_COPIES),
        compiler_params=pltpu.CompilerParams(collective_id=ident, has_side_effects=True, vmem_limit_bytes=60 << 20),
        name="forward",
    )(mix, a1, dcol, drow, th, tl, group, qkv_w, out_w, x, dy, gain, gu, w_down)


def ffn_call(a2, first, second, gu_w, down_w):
    count, w = a2.shape
    half = down_w.shape[0]
    m = count // 4
    part = half // 2

    def body(a2_ref, df1_ref, df2_ref, gw_ref, dw_ref, dgu_ref, hid_ref, gd_ref, df_ref, total):
        step = pl.program_id(0)

        @pl.when(step == 0)
        def _():
            total[...] = jnp.zeros_like(total)

        q = m // 4
        for i in range(2):
            df_ref[2 * i * q : (2 * i + 1) * q] = df1_ref[i * q : (i + 1) * q]
            df_ref[(2 * i + 1) * q : (2 * i + 2) * q] = df2_ref[i * q : (i + 1) * q]
        for j in range(2):
            cols, more = slice(j * part, (j + 1) * part), slice(half + j * part, half + (j + 1) * part)
            gate, up_act = dot(a2_ref[...], gw_ref[:, cols]), dot(a2_ref[...], gw_ref[:, more])
            dhidden = dot(df_ref[...], dw_ref[cols], 1, 1)
            sig = jax.nn.sigmoid(gate)
            silu = gate * sig
            hid_ref[:, cols] = (silu * up_act).astype(bf16)
            dgu_ref[:, cols] = (dhidden * up_act * sig * (1.0 + gate * (1.0 - sig))).astype(bf16)
            dgu_ref[:, more] = (dhidden * silu).astype(bf16)
        total[...] += dot(hid_ref[...], df_ref[...], 0, 0)

        @pl.when(step == 3)
        def _():
            gd_ref[...] = total[...].astype(bf16)

    row = lambda k, m=m: pl.BlockSpec((m, k), lambda i: (i, 0))
    full = lambda v: pl.BlockSpec(v.shape, lambda i: (0, 0), pipeline_mode=pl.Buffered(1))
    return pl.pallas_call(
        body,
        grid=(4,),
        in_specs=[row(w), row(w, m // 2), row(w, m // 2), full(gu_w), full(down_w)],
        out_specs=[row(2 * half), row(half), pl.BlockSpec((half, w), lambda i: (0, 0))],
        out_shape=[shape((count, 2 * half), bf16), shape((count, half), bf16), shape((half, w), bf16)],
        scratch_shapes=[pltpu.VMEM((m, w), bf16), pltpu.VMEM((half, w), f32)],
        compiler_params=pltpu.CompilerParams(vmem_limit_bytes=40 << 20),
        name="ffn",
    )(a2, first, second, gu_w, down_w)


def mid_back_call(dgu, gu_w, a2, hidden, down_w, dy, resid, gain, down, ident):
    n, w = dy.shape
    m, half = dgu.shape[0] // 4, gu_w.shape[1] // 2

    def body(dgu_ref, gw_ref, a2_ref, hid_ref, dw_ref, dy_ref, r_ref, g_ref, down_ref,
             dresid_ref, out_ref, sum_ref, down_out, gate_out, up_out, op_out,
             parts, a2s, hids, dws, stage, gates, v, local, rc, rd, rx, ry, td, tx, ty, d_got, d_made, g_got, g_made, send, recv):
        net = Net()
        sems = (send, recv)
        net.greet("xyc")
        base = SCATTER_COPIES + GATHER_COPIES
        line_d = ScatterLine(net, down_ref, d_got, d_made, sems, base)
        line_g = ScatterLine(net, gates, g_got, g_made, sems, base + LINE_COPIES)
        line_d.step(0)
        loads = [pltpu.make_async_copy(src, dst, local.at[i]) for i, (src, dst) in enumerate(((a2_ref, a2s), (hid_ref, hids), (dw_ref, dws)))]
        for copy in loads:
            copy.start()
        A, B = pl.ds(0, n // 2), pl.ds(n // 2, n // 2)
        go = {}

        def part(chip):
            for j in range(3):
                cols = slice(j * (w // 3), (j + 1) * (w // 3))
                total = dot(dgu_ref[chip * m : (chip + 1) * m], gw_ref[cols], 1, 1)
                parts[chip, :, :, cols] = total.astype(bf16).reshape(2, n, w // 3)

        def swap(chip, i):
            go[chip] = Later(lambda: net.copy(parts.at[chip, 1], rc.at[chip], sems, i, "c"))

        def add(dst, chip, start, more=None):
            def one(r):
                total = wide(parts[chip, 0, r]) + wide(rc[chip, r])
                if more is not None:
                    total = total + wide(more[r])
                dst[r] = total.astype(bf16)

            tiles(start, n // 2, one)

        def weights(first, last):
            for i in range(first, last):
                rows = slice(i * (w // 4), (i + 1) * (w // 4))
                total = dot(a2s[:, rows], dgu_ref[...], 0, 0)
                gates[i] = total[:, :half].astype(bf16)
                up_out[i] = total[:, half:].astype(bf16)

        def put_back(chip):
            return pltpu.make_async_copy(stage.at[chip % 2], op_out.at[chip], local.at[4 + chip % 2])

        def forward(chip):
            if chip >= 2:
                put_back(chip - 2).wait()
            for j in range(3):
                cols = slice(j * (w // 3), (j + 1) * (w // 3))
                total = dot(hids[chip * m : (chip + 1) * m], dws[:, cols])
                stage[chip % 2, :, :, cols] = total.astype(bf16).reshape(2, n, w // 3)
            put_back(chip).start()

        part(3)
        swap(3, 0)
        part(2)
        swap(2, 2)
        go[3].wait_recv()
        add(td, 3, 0)
        go["dA"] = Later(lambda: net.copy(td.at[A], rd.at[A], sems, 4, "x"))
        add(td, 3, n // 2)
        go["dB"] = Later(lambda: net.copy(td.at[B], rd.at[B], sems, 5, "y"))
        part(1)
        swap(1, 1)
        go[2].wait_recv()
        add(ty, 2, n // 2)
        go["yB"] = Later(lambda: net.copy(ty.at[B], ry.at[B], sems, 7, "y"))
        part(0)
        swap(0, 3)
        go[1].wait_recv()
        add(tx, 1, 0)
        go["xA"] = Later(lambda: net.copy(tx.at[A], rx.at[A], sems, 6, "x"))
        loads[0].wait()
        go["dA"].wait_recv()
        add(ty, 2, 0, rd)
        go["yA"] = Later(lambda: net.copy(ty.at[A], ry.at[A], sems, 8, "y"))
        go["dB"].wait_recv()
        add(tx, 1, n // 2, rd)
        go["xB"] = Later(lambda: net.copy(tx.at[B], rx.at[B], sems, 9, "x"))
        weights(0, 4)
        line_g.step(0)
        line_d.step(1)
        loads[1].wait()
        loads[2].wait()
        sum_ref[...] = jnp.zeros_like(sum_ref)
        go[0].wait_recv()

        def ready(side):
            for name in (("xA", "yA"), ("xB", "yB"))[side]:
                go[name].wait_recv()

            def rows_of(r):
                da2 = wide(parts[0, 0, r]) + wide(rc[0, r]) + wide(rx[r]) + wide(ry[r])
                res = r_ref[r]
                inv = lax.rsqrt(jnp.mean(res * res, axis=1, keepdims=True) + 1e-06)
                unit = res * inv
                sum_ref[0:1] += jnp.sum(da2 * unit, axis=0, keepdims=True)
                dn = da2 * g_ref[...]
                dresid = wide(dy_ref[r]) + inv * (dn - unit * inv * jnp.mean(dn * res, axis=1, keepdims=True))
                dresid_ref[r] = dresid
                v[r] = dresid.astype(bf16)

            tiles(side * (n // 2), n // 2, rows_of)

        poll, drain = polls(
            lambda: (forward(0), forward(1)), lambda: (line_d.step(2), line_g.step(1)), lambda: (forward(2), forward(3)), lambda: line_g.step(2)
        )
        gather_rows(net, v, out_ref, sems, SCATTER_COPIES, ready, poll)
        drain()
        last = pltpu.make_async_copy(v, out_ref.at[0, 0], local.at[3])
        last.start()

        def put(ref):
            def store(r, total):
                ref[r] = total.astype(bf16)

            return store

        line_d.finish(put(down_out))
        line_g.finish(put(gate_out))
        for copy in go.values():
            copy.wait_send()
        put_back(2).wait()
        put_back(3).wait()
        last.wait()

    return comm_call(
        body, "mid_back", ident, (dgu, gu_w, a2, hidden, down_w, dy, resid, gain, down), [VM] * 2 + [ANY] * 3 + [VM] * 4,
        [shape((n, w), f32), shape((4, 2, n, w), bf16), shape((8, w), f32), shape(down.shape[1:], bf16), shape((w // 4, half), bf16),
         shape((4, w // 4, half), bf16), shape((4, 2, n, w), bf16)],
        [VM, ANY, VM, VM, VM, VM, ANY],
        [pltpu.VMEM((4, 2, n, w), bf16), pltpu.VMEM(a2.shape, bf16), pltpu.VMEM(hidden.shape, bf16), pltpu.VMEM(down_w.shape, bf16),
         pltpu.VMEM((2, 2, n, w), bf16), pltpu.VMEM((4, w // 4, half), bf16), pltpu.VMEM((n, w), bf16), pltpu.SemaphoreType.DMA((6,))]
        + scatter_scratch(n, w) + line_scratch(*down.shape[1:]) + line_scratch(w // 4, half)
        + dma_sems(SCATTER_COPIES + GATHER_COPIES + 2 * LINE_COPIES),
    )


class Home:
    def __init__(self, net, zq, cq, fq, sems, base):
        self.net, self.zq, self.cq, self.fq, self.sems, self.base = net, zq, cq, fq, sems, base
        self.r = cq.shape[2]

    def rows(self, i, j):
        return pl.ds(pl.multiple_of((2 * i + j) * self.r, self.r), self.r)

    def over_c(self, i):
        net = self.net
        return net.copy(self.zq.at[self.rows(i, 1 - net.c)], self.cq.at[i, net.c], self.sems, self.base + i, "c")

    def over_y(self):
        net = self.net
        return net.copy(self.cq.at[1 - net.y], self.fq.at[net.x, net.y], self.sems, self.base + 2, "y")

    def over_x(self):
        net = self.net
        return net.copy(self.fq.at[net.x], self.fq.at[net.x], self.sems, self.base + 3, "x")

    def step(self, d):
        net = self.net
        if d == 0:
            for i in range(2):
                self.over_c(i).start()
                self.cq[i, net.c] = self.zq[self.rows(i, net.c)]
        elif d == 1:
            for i in range(2):
                self.over_c(i).wait_recv()
            self.over_y().start()
            self.fq[net.x, net.y] = self.cq[net.y]
        elif d == 2:
            self.over_y().wait_recv()
            self.over_x().start()
        else:
            self.over_x().wait_recv()

    def finish(self):
        for i in range(2):
            self.over_c(i).wait_send()
        self.over_y().wait_send()
        self.over_x().wait_send()

    def spread(self, dst):
        for i in range(2):
            for k in range(4):
                for m in range(4):
                    col = 256 * (4 * m + k) + 128 * i
                    dst[:, col : col + 128] = wide(self.fq[i, k // 2, k % 2, :, m * 128 : (m + 1) * 128])


HOME_COPIES = 4


def home_scratch(r, k):
    return [pltpu.VMEM((2, 2, r, k), bf16), pltpu.VMEM((2, 2, 2, r, k), bf16)]


def end_call(da_parts, qkv, wo, gate_up, small, x, dresid, gain, ident):
    n, w = da_parts.shape[2:]
    rows, wide_q = qkv.shape[2] // 4, qkv.shape[3]

    def body(da_ref, q_ref, wo_ref, up_ref, small_ref, x_ref, dresid_ref, g_ref,
             gx_ref, gq_ref, go_ref, gu_ref, total_ref,
             rc, rd, rx, ry, td, tx, ty, q_got, q_made, zq, cq, fq, cu, fu, ro, s_got, s_sum, s_line, send, recv):
        net = Net()
        sems = (send, recv)
        net.greet("xyc")
        base = SCATTER_COPIES
        lines = [ScatterLine(net, q_ref.at[i], q_got.at[i], q_made.at[i], sems, base + 6 * i) for i in range(2)]
        line_s = GatherLine(net, s_sum.at[2], s_line, sems, base + 12)
        base += 18
        homes = [Home(net, zq.at[i], cq.at[i], fq.at[i], sems, base + 4 * i) for i in range(2)]
        home_u = Home(net, up_ref, cu, fu, sems, base + 8)
        base += 12
        for line in lines:
            line.step(0)
        hops = [net.send(small_ref, s_got.at[0], sems, base, "c")]
        home_u.step(0)

        def small_step(i):
            hops[i].wait_recv()
            s_sum[i] = (small_ref[...] if i == 0 else s_sum[i - 1]) + s_got[i]
            if i < 2:
                hops.append(net.send(s_sum.at[i], s_got.at[i + 1], sems, base + 1 + i, "yx"[i]))
            else:
                line_s.step(0)

        scatter = scatter_steps(net, da_ref, rc, rd, rx, ry, td, tx, ty, sems, 0)
        next(scatter)
        small_step(0)
        next(scatter)
        home_u.step(1)
        swap_o = net.send(wo_ref, ro, sems, base + 3, "x")
        lines[0].step(1)
        small_step(1)
        done = next(scatter)
        lines[1].step(1)
        home_u.step(2)
        small_step(2)
        lines[0].step(2)
        line_s.step(1)
        lines[1].step(2)
        line_s.step(2)
        for half in range(2):
            done(half)

            def rows_of(at):
                da = wide(da_ref[0, 0, at]) + wide(rc[0, at]) + wide(rx[at]) + wide(ry[at])
                xf = wide(x_ref[at])
                r = lax.rsqrt(jnp.mean(xf * xf, axis=1, keepdims=True) + 1e-06)
                dn = da * g_ref[...]
                gx_ref[at] = dresid_ref[at] + r * (dn - xf * r * r * jnp.mean(dn * xf, axis=1, keepdims=True))

            tiles(half * (n // 2), n // 2, rows_of)

        for i in range(2):

            def put(at, total):
                zq[i, at] = total.astype(bf16)

            lines[i].finish(put)
            homes[i].step(0)
        homes[0].step(1)
        homes[1].step(1)
        homes[0].step(2)
        homes[1].step(2)
        line_s.step(3)
        s_line[net.z] = s_sum[2]
        total_ref[...] = (s_line[0] + s_line[1]) + (s_line[2] + s_line[3])
        swap_o.wait_recv()
        go_ref[...] = wide(wo_ref[...]) + wide(ro[...])
        home_u.step(3)
        home_u.spread(gu_ref)
        for part in range(2):
            homes[part].step(3)
            for i in range(2):
                for k in range(4):
                    pair = 4 * i + 2 * (k % 2) + k // 2
                    for m in range(3):
                        to = 3 * part + m
                        col = (to // 2) * MODEL_WIDTH + (2 * pair + to % 2) * E
                        gq_ref[:, col : col + E] = wide(fq[part, i, k // 2, k % 2, :, m * EP : m * EP + E])
        line_s.finish()
        for home in homes + [home_u]:
            home.finish()
        for copy in hops + [swap_o]:
            copy.wait_send()

    two = lambda specs: [pltpu.VMEM((2,) + v.shape, v.dtype) for v in specs]
    return comm_call(
        body, "end", ident, (da_parts, qkv, wo, gate_up, small, x, dresid, gain), [VM] * 8,
        [shape((n, w), f32), shape((rows, 3 * MODEL_WIDTH), f32), shape(wo.shape, f32), shape((rows, FF), f32), shape(small.shape, f32)],
        [VM] * 5,
        scatter_scratch(n, w) + two(line_scratch(4 * rows, wide_q)) + two([pltpu.VMEM((4 * rows, wide_q), bf16)])
        + two(home_scratch(rows, wide_q)) + home_scratch(rows, FF // 8) + [pltpu.VMEM(wo.shape, bf16)]
        + [pltpu.VMEM((3,) + small.shape, f32), pltpu.VMEM((3,) + small.shape, f32), pltpu.VMEM((4,) + small.shape, f32)]
        + dma_sems(SCATTER_COPIES + 18 + 12 + 4),
    )


def back_call(mix, qkv, dcol, drow, tt, gain, dattn, xhat, s, p, z, a1, out_w, qkv_w, out_parts, up_parts, wo, gate, down, resid, ident):
    rows, t, _ = qkv.shape
    n, w = out_parts.shape[2:]
    rows_o, rows_d, wide_q = wo.shape[1], down.shape[0], 3 * EP

    def body(mix_ref, qkv_ref, dcol_ref, drow_ref, tt_ref, gain_ref, dattn_ref, xhat_ref, s_ref, p_ref, z_ref, a1_ref,
             ow_ref, qw_ref, op_ref, gu_ref, wo_ref, gate_ref, down_ref, resid_ref,
             da_ref, q16_ref, sum_ref, gconv_ref, gmix_ref, gg_ref, out_ref, gu_out, go_out, gg_out, gd_ref,
             m_ref, gq_ref, dq, rc, rd, rx, ry, td, tx, ty, g_got, g_made, o_got, o_made, po, cg, fg, fd, send, recv):
        net = Net()
        sems = (send, recv)
        step = pl.program_id(0)
        base = SCATTER_COPIES
        line = ScatterLine(net, gu_ref, g_got, g_made, sems, base)
        line_o = ScatterLine(net, po, o_got, o_made, sems, base + 6)
        home = Home(net, gate_ref, cg, fg, sems, base + 12)
        x, c = net.x, net.c
        to_c = lambda: net.copy(wo_ref.at[1 - c], po.at[2 * x + c], sems, base + 16, "c")
        to_x = lambda: net.copy(down_ref, fd.at[x], sems, base + 17, "x")
        scatter = scatter_steps(net, op_ref, rc, rd, rx, ry, td, tx, ty, sems, 0)

        @pl.when(step == 0)
        def _():
            net.greet("xyc")
            line.step(0)
            to_c().start()
            next(scatter)
            home.step(0)
            po[2 * (1 - x)] = jnp.zeros((rows_o, w), bf16)
            po[2 * (1 - x) + 1] = jnp.zeros((rows_o, w), bf16)
            po[2 * x + c] = wo_ref[c]
            fd[x] = down_ref[...]
            m_ref[...] = jnp.zeros_like(m_ref)
            gmix_ref[...] = jnp.zeros_like(gmix_ref)
            gg_ref[...] = jnp.zeros_like(gg_ref)
            gq_ref[...] = jnp.zeros_like(gq_ref)

        allowed = allowed_mask(dcol_ref[0], drow_ref[0])
        scale = 1.0 / math.sqrt(E)
        lane = lax.broadcasted_iota(jnp.int32, (1, EP), 1)
        prob = [p_ref[0, 0], p_ref[0, 1]]
        dmixed = []
        for h in range(2):
            cols = slice(h * EP, (h + 1) * EP)
            dn, xh = dot(dattn_ref[0], ow_ref[cols], 1, 1), xhat_ref[0, :, cols]
            gg_ref[0:1, cols] += jnp.sum(dn * xh, axis=0, keepdims=True)
            dc = dn * gain_ref[0:1, cols]
            m1 = jnp.sum(dc, axis=1, keepdims=True) / E
            m2 = jnp.sum(dc * xh, axis=1, keepdims=True) / E
            dh = jnp.where(lane < E, s_ref[0, :, cols] * (dc - m1 - xh * m2), 0.0).astype(bf16)
            v = qkv_ref[0, :, (4 + h) * EP : (5 + h) * EP]
            mixed = (mix_ref[h, 0] * prob[0] + mix_ref[h, 1] * prob[1]).astype(bf16)
            dmixed.append(dot(dh, v, 1, 1))
            dq[:, (4 + h) * EP : (5 + h) * EP] = dot(mixed, dh, 0, 0).astype(bf16)
        for h in range(2):
            for c in range(2):
                r = 2 * h + c
                gmix_ref[r : r + 1, :] += jnp.sum(dmixed[h] * prob[c], axis=0, keepdims=True)
        for c in range(2):
            dp = mix_ref[0, c] * dmixed[0] + mix_ref[1, c] * dmixed[1]
            dconv = prob[c] * (dp - jnp.sum(dp * prob[c], axis=1, keepdims=True))
            ahead = jnp.concatenate([up(dconv, a).astype(bf16) for a in range(QWIN)], 1)
            m_ref[c] += dot(z_ref[0, c], ahead, 0, 0)
            ds = jnp.where(allowed, dot(ahead, tt_ref[c]), 0.0).astype(bf16)
            q = qkv_ref[0, :, c * EP : (c + 1) * EP]
            k = qkv_ref[0, :, (2 + c) * EP : (3 + c) * EP]
            dq[:, c * EP : (c + 1) * EP] = (dot(ds, k) * scale).astype(bf16)
            dq[:, (2 + c) * EP : (3 + c) * EP] = (dot(ds, q, 0, 0) * scale).astype(bf16)
        da_ref[0] = dot(dq[...], qw_ref[...], 1, 1).astype(bf16)
        for i in range(0, w, 384):
            gq_ref[i : i + 384] += dot(a1_ref[0, :, i : i + 384], dq[...], 0, 0)

        done = []

        @pl.when(step == 1)
        def _():
            next(scatter)
            to_c().wait_recv()
            line_o.step(0)
            home.step(1)
            to_x().start()

        @pl.when(step == 2)
        def _():
            line.step(1)
            done.append(next(scatter))

        @pl.when(step == 3)
        def _():
            line_o.step(1)
            home.step(2)

        @pl.when(step == 4)
        def _():
            line.step(2)

        @pl.when(step == 5)
        def _():
            line_o.step(2)

        @pl.when(step == rows - 1)
        def _():
            lanes = lax.broadcasted_iota(jnp.int32, (8, t), 1)
            for h in range(2):
                for a in range(QWIN):
                    total = jnp.zeros((8, t), f32)
                    for first in range(0, t, 8):
                        part = m_ref[h, first : first + 8, a * t : (a + 1) * t]
                        turned = pltpu.roll(part, t - first, 1) if first else part
                        total = total + jnp.where(lanes < t - first, turned, 0.0)
                    gconv_ref[h, a] = total[:, :EP]
            for half in range(2):
                done[0](half)

                def sum_of(at):
                    total = wide(op_ref[0, 0, at]) + wide(rc[0, at]) + wide(rx[at]) + wide(ry[at])
                    out_ref[at] = (resid_ref[at] + total).astype(bf16)

                tiles(half * (n // 2), n // 2, sum_of)

            def put(at, total):
                gu_out[at] = total.astype(bf16)

            line.finish(put)

            def put_o(at, total):
                go_out[at] = total.astype(bf16)

            line_o.finish(put_o)
            to_x().wait_recv()
            for i in range(2):
                gd_ref[i * rows_d : (i + 1) * rows_d] = wide(fd[i])
            home.step(3)
            home.spread(gg_out)
            home.finish()
            to_x().wait_send()
            to_c().wait_send()
            for i in range(0, w, 384):
                part = gq_ref[i : i + 384]
                for j in range(2):
                    q16_ref[j, i : i + 384] = part[:, j * wide_q : (j + 1) * wide_q].astype(bf16)
                sum_ref[:, i : i + 384] = lax.dot_general(
                    jnp.ones((8, 6 * EP), f32), part * wide(qw_ref[i : i + 384]), (((1,), (1,)), ((), ())),
                    precision=lax.Precision.HIGHEST, preferred_element_type=f32,
                )

    row = lambda *sh: pl.BlockSpec((1,) + sh, lambda i: (i,) + (0,) * len(sh))
    full = lambda v: pl.BlockSpec(v.shape, lambda i: (0,) * v.ndim, pipeline_mode=pl.Buffered(1))
    keep = lambda *sh: pl.BlockSpec(sh, lambda i: (0,) * len(sh))
    return pl.pallas_call(
        body,
        grid=(rows,),
        in_specs=[pl.BlockSpec(memory_space=pltpu.SMEM), row(t, 6 * EP), row(t, 1), row(1, t), full(tt), full(gain),
                  row(t, w), row(t, 2 * EP), row(t, 2 * EP), row(2, t, t), row(2, t, t), row(t, w),
                  full(out_w), full(qkv_w), full(out_parts), full(up_parts), full(wo), full(gate), full(down), full(resid)],
        out_specs=[row(t, w), keep(2, w, wide_q), keep(8, w), keep(2, QWIN, 8, EP), keep(8, t), keep(8, 2 * EP), keep(n, w),
                   keep(*up_parts.shape[1:]), keep(rows_o, w), keep(rows_o, FF), keep(2 * rows_d, w)],
        out_shape=[
            shape((rows, t, w), bf16),
            shape((2, w, wide_q), bf16),
            shape((8, w), f32),
            shape((2, QWIN, 8, EP), f32),
            shape((8, t), f32),
            shape((8, 2 * EP), f32),
            shape((n, w), bf16),
            shape(up_parts.shape[1:], bf16),
            shape((rows_o, w), bf16),
            shape((rows_o, FF), f32),
            shape((2 * rows_d, w), f32),
        ],
        scratch_shapes=[pltpu.VMEM((2, t, QWIN * t), f32), pltpu.VMEM((w, 6 * EP), f32), pltpu.VMEM((t, 6 * EP), bf16)] + scatter_scratch(n, w)
        + line_scratch(*up_parts.shape[1:]) + line_scratch(rows_o, w) + [pltpu.VMEM((4, rows_o, w), bf16)]
        + home_scratch(rows_o, FF // 8) + [pltpu.VMEM((2, rows_d, w), bf16)] + dma_sems(SCATTER_COPIES + 18),
        compiler_params=pltpu.CompilerParams(collective_id=ident, has_side_effects=True, vmem_limit_bytes=63 << 20),
        name="back",
    )(mix, qkv, dcol, drow, tt, gain, dattn, xhat, s, p, z, a1, out_w, qkv_w, out_parts, up_parts, wo, gate, down, resid)


def rms_scale(values):
    return lax.rsqrt(jnp.mean(values * values, axis=1, keepdims=True) + 1e-06)


class Links:
    def __init__(self, fsdp):
        self.fsdp = fsdp
        index = lax.axis_index("fsdp")
        self.x = lax.axis_index("rep")
        self.z, self.y, self.c = index // 4, (index // 2) % 2, index % 2

    def across(self, flip, v):
        if flip == "x":
            return lax.ppermute(v, "rep", [(0, 1), (1, 0)])
        bit = {"y": 2, "c": 1}[flip]
        return lax.ppermute(v, "fsdp", [(f, f ^ bit) for f in range(self.fsdp)])

    def along(self, v, step):
        pairs = [(f, f + 4 * step) for f in range(self.fsdp) if 0 <= f + 4 * step < self.fsdp]
        return lax.ppermute(v, "fsdp", pairs)

    def ordered(self, bit, mine, other, axis):
        first, second = jnp.where(bit == 0, mine, other), jnp.where(bit == 0, other, mine)
        return jnp.stack([first, second], axis)

    def gather_z(self, v):
        left, right = [], []
        a = b = v
        for _ in range(3):
            a, b = self.along(a, 1), self.along(b, -1)
            left.append(a)
            right.append(b)
        line = jnp.stack(left[::-1] + [v] + right)
        return lax.dynamic_slice_in_dim(line, 3 - self.z, 4, 0)

    def scatter_z(self, parts):
        zero = jnp.zeros((3,) + parts.shape[1:], parts.dtype)
        line = lax.dynamic_slice_in_dim(jnp.concatenate([zero, parts, zero]), self.z, 7, 0)
        low = lambda v: v.astype(bf16)
        a = self.along(low(line[6]), 1)
        b = self.along(low(line[0]), -1)
        for step in (1, 2):
            a = self.along(low(line[6 - step] + a.astype(f32)), 1)
            b = self.along(low(line[step] + b.astype(f32)), -1)
        return line[3] + a.astype(f32) + b.astype(f32)

    def gather_plane(self, v):
        n = v.shape[0] // 2
        vx, vy = self.across("x", v), self.across("y", v)
        vd = jnp.concatenate([self.across("y", vx[:n]), self.across("x", vy[n:])])
        return [jnp.concatenate([u, self.across("c", u)]) for u in (v, vx, vy, vd)]

    def scatter_plane(self, parts):
        low = lambda v: v.astype(bf16)
        n = parts[0].shape[0] // 2
        s = [p[:n] + self.across("c", low(p[n:])).astype(f32) for p in parts]
        m = n // 2
        dx, dy = self.across("x", low(s[3][:m])), self.across("y", low(s[3][m:]))
        to_x = jnp.concatenate([s[1][:m], s[1][m:] + dy.astype(f32)])
        to_y = jnp.concatenate([s[2][:m] + dx.astype(f32), s[2][m:]])
        return s[0] + self.across("x", low(to_x)).astype(f32) + self.across("y", low(to_y)).astype(f32)


class Weights:
    def __init__(self, links):
        self.links = links
        self.line = links.fsdp == 16
        x, y, c = links.x, links.y, links.c
        self.pair = 4 * x + 2 * c + y
        self.slot = 4 * x + 2 * y + c

    def spread(self, shard, dims):
        l = self.links
        ax, ay, ac = dims
        v = lax.dynamic_index_in_dim(shard, l.x, ax, keepdims=True)
        keep = lax.dynamic_index_in_dim(v, l.y, ay, keepdims=True)
        sent = l.across("y", lax.dynamic_index_in_dim(v, 1 - l.y, ay, keepdims=True))
        v = l.ordered(l.y, keep, sent, 0)
        keep = lax.dynamic_index_in_dim(v, l.c, ac + 1, keepdims=True)
        sent = l.across("c", lax.dynamic_index_in_dim(v, 1 - l.c, ac + 1, keepdims=True))
        v = l.ordered(l.c, keep, sent, 1)
        return l.gather_z(v)

    def collect(self, grad, dims):
        l = self.links
        ax, ay, ac = dims
        low = lambda v: v.astype(bf16)
        v = l.scatter_z(grad)
        keep = lax.dynamic_index_in_dim(v, l.c, 1, keepdims=False)
        sent = l.across("c", low(lax.dynamic_index_in_dim(v, 1 - l.c, 1, keepdims=False)))
        v = self.join(l.c, keep, sent.astype(f32), ac + 1)
        keep = lax.dynamic_index_in_dim(v, l.y, 0, keepdims=False)
        sent = l.across("y", low(lax.dynamic_index_in_dim(v, 1 - l.y, 0, keepdims=False)))
        v = low(self.join(l.y, keep, sent.astype(f32), ay))
        return self.join(l.x, v, l.across("x", v), ax).astype(f32)

    def join(self, bit, mine, other, axis):
        first, second = jnp.where(bit == 0, mine, other), jnp.where(bit == 0, other, mine)
        return jnp.concatenate([first, second], axis)

    def whole(self, shard):
        return lax.all_gather(shard, "fsdp", axis=0, tiled=True)

    def owned(self, grad):
        part = lax.psum_scatter(grad, "fsdp", scatter_dimension=0, tiled=True)
        return lax.psum(part.astype(bf16), "rep").astype(f32)

    def qkv(self, shard):
        rows = shard.shape[0]
        if self.line:
            v = self.spread(shard.reshape(rows, 3, 2, 2, 2, 2 * E), (2, 4, 3))
            v = v.reshape(MODEL_WIDTH, 3, 2, E)
        else:
            v = self.whole(shard).reshape(MODEL_WIDTH, 3, 8, 2, E)
            v = lax.dynamic_index_in_dim(v, self.pair, 2, keepdims=False)
        return jnp.pad(v, ((0, 0), (0, 0), (0, 0), (0, EP - E))).reshape(MODEL_WIDTH, 6 * EP)

    def qkv_back(self, grad):
        g = grad.reshape(MODEL_WIDTH, 3, 2, EP)[..., :E]
        if self.line:
            return self.collect(g.reshape(4, 2, 2, -1, 3, 1, 1, 1, 2 * E), (2, 4, 3)).reshape(-1, 3 * MODEL_WIDTH)
        zero = jnp.zeros((MODEL_WIDTH, 3, 8, 2, E), f32)
        return self.owned(lax.dynamic_update_index_in_dim(zero, g, self.pair, 2).reshape(MODEL_WIDTH, 3 * MODEL_WIDTH))

    def out(self, shard):
        l = self.links
        if self.line:
            v = l.gather_z(shard)
            keep = lax.dynamic_index_in_dim(v, 2 * l.x + l.c, 0, keepdims=False)
            sent = l.across("c", lax.dynamic_index_in_dim(v, 2 * l.x + 1 - l.c, 0, keepdims=False))
            v = l.ordered(l.c, keep, sent, 0)
        else:
            v = self.whole(shard).reshape(8, 2, E, MODEL_WIDTH)
            v = lax.dynamic_index_in_dim(v, self.pair, 0, keepdims=False)
        return jnp.pad(v, ((0, 0), (0, EP - E), (0, 0))).reshape(2 * EP, MODEL_WIDTH)

    def out_back(self, grad):
        l = self.links
        g = grad.reshape(2, EP, MODEL_WIDTH)[:, :E]
        if self.line:
            keep = lax.dynamic_index_in_dim(g, l.c, 0, keepdims=False)
            sent = l.across("c", lax.dynamic_index_in_dim(g, 1 - l.c, 0, keepdims=False).astype(bf16)).astype(f32)
            at = jnp.arange(4)[:, None, None]
            parts = jnp.where(at == 2 * l.x + l.c, keep[None], jnp.where(at == 2 * l.x + 1 - l.c, sent[None], 0.0))
            v = l.scatter_z(parts).astype(bf16)
            return (v + l.across("x", v)).astype(f32)
        zero = jnp.zeros((8, 2, E, MODEL_WIDTH), f32)
        return self.owned(lax.dynamic_update_index_in_dim(zero, g, self.pair, 0).reshape(MODEL_WIDTH, MODEL_WIDTH))

    def ffn_in(self, gate, up_):
        rows = gate.shape[0]
        both = jnp.stack([gate, up_], 1)
        if self.line:
            v = self.spread(both.reshape(rows, 2, 4, 2, 2, 2, FF // 32), (5, 3, 4))
            return v.reshape(MODEL_WIDTH, FF // 4)
        v = self.whole(both).reshape(MODEL_WIDTH, 2, 8, FF // 8)
        return lax.dynamic_index_in_dim(v, self.slot, 2, keepdims=False).reshape(MODEL_WIDTH, FF // 4)

    def ffn_in_back(self, grad):
        if self.line:
            v = self.collect(grad.reshape(4, 2, 2, -1, 2, 4, 1, 1, 1, FF // 32), (5, 3, 4)).reshape(-1, 2, FF)
        else:
            zero = jnp.zeros((MODEL_WIDTH, 2, 8, FF // 8), f32)
            g = grad.reshape(MODEL_WIDTH, 2, FF // 8)
            v = self.owned(lax.dynamic_update_index_in_dim(zero, g, self.slot, 2).reshape(MODEL_WIDTH, 2, FF))
        return v[:, 0], v[:, 1]

    def ffn_out(self, shard):
        l = self.links
        if self.line:
            v = lax.dynamic_index_in_dim(shard.reshape(2, FF // 32, MODEL_WIDTH), l.x, 0, keepdims=False)
            return l.gather_z(v).reshape(FF // 8, MODEL_WIDTH)
        v = self.whole(shard).reshape(8, FF // 8, MODEL_WIDTH)
        return lax.dynamic_index_in_dim(v, self.slot, 0, keepdims=False)

    def ffn_out_back(self, grad):
        l = self.links
        if self.line:
            v = l.scatter_z(grad.reshape(4, FF // 32, MODEL_WIDTH)).astype(bf16)
            return self.join(l.x, v, l.across("x", v), 0).astype(f32)
        zero = jnp.zeros((8, FF // 8, MODEL_WIDTH), f32)
        return self.owned(lax.dynamic_update_index_in_dim(zero, grad, self.slot, 0).reshape(FF, MODEL_WIDTH))

    def gains(self, *shards):
        l = self.links
        v = jnp.stack(shards)
        if self.line:
            v = l.ordered(l.c, v, l.across("c", v), 0)
            v = l.ordered(l.y, v, l.across("y", v), 0)
            v = l.gather_z(v)
            v = v.reshape(16, len(shards), -1).transpose(1, 0, 2).reshape(len(shards), MODEL_WIDTH)
        else:
            v = lax.all_gather(v, "fsdp", axis=1, tiled=True)
        return [v[i].astype(f32) for i in range(len(shards))]


def per_device(
    fsdp,
    x_in,
    doc_ids,
    w_qkv,
    w_out,
    gain_attn,
    gain_group,
    conv_kernel,
    head_mix,
    gain_ffn,
    w_gate,
    w_up,
    w_down,
    cotangent,
):
    links = Links(fsdp)
    weights = Weights(links)
    tokens = x_in.shape[1]

    x_all = jnp.concatenate(links.gather_plane(x_in[0]))
    qkv_w = weights.qkv(w_qkv)
    gain_a, gain_g, gain_f = weights.gains(gain_attn, gain_group, gain_ffn)
    docs = doc_ids
    for flip in ("y", "x"):
        docs = jnp.concatenate([docs, links.across(flip, docs)])
    docs = jnp.stack([docs, links.across("c", docs)], 1)
    docs = docs[jnp.array([0, 2, 1, 3])].reshape(8, tokens)
    out_w = weights.out(w_out)
    in_w = weights.ffn_in(w_gate, w_up)
    down_w = weights.ffn_out(w_down)
    upstream_chips = links.gather_plane(cotangent[0])

    kernel = lax.dynamic_slice_in_dim(conv_kernel, 2 * weights.pair, 2, 0)
    mix = lax.dynamic_slice_in_dim(head_mix, 2 * weights.pair, 2, 0)
    th, tl, tt = bands(kernel, tokens)
    group = lax.dynamic_slice_in_dim(gain_g.reshape(8, 2, E), weights.pair, 1, 0)
    group = jnp.pad(group, ((0, 0), (0, 0), (0, EP - E))).reshape(1, 2 * EP)
    doc_col, doc_row = docs[:, :, None], docs[:, None, :]

    xf_all = x_all.astype(f32)
    a1 = (xf_all * rms_scale(xf_all) * gain_a).astype(bf16)
    qkv = dot(a1, qkv_w).astype(bf16).reshape(8, tokens, 6 * EP)
    normed, xhat, s, probs, zeroed = attend(mix, qkv, doc_col, doc_row, th, tl, group)
    normed = normed.reshape(4, 2 * tokens, 2 * EP)
    xf = x_in[0].astype(f32)
    resid = xf + links.scatter_plane([dot(normed[i], out_w) for i in range(4)])

    r2 = rms_scale(resid)
    a2_chips = links.gather_plane((resid * r2 * gain_f).astype(bf16))
    out_parts, back_parts, hiddens, dgus = [], [], [], []
    half = FF // 8
    for a2, dffn in zip(a2_chips, upstream_chips):
        gu = dot(a2, in_w)
        gate, up_act = gu[:, :half], gu[:, half:]
        sig = jax.nn.sigmoid(gate)
        silu = gate * sig
        hidden = (silu * up_act).astype(bf16)
        dhidden = dot(dffn, down_w, 1, 1)
        dgate = (dhidden * up_act * sig * (1.0 + gate * (1.0 - sig))).astype(bf16)
        dup = (dhidden * silu).astype(bf16)
        dgu = jnp.concatenate([dgate, dup], 1)
        hiddens.append(hidden)
        dgus.append(dgu)
        back_parts.append(dot(dgu, in_w, 1, 1))
        out_parts.append(dot(hidden, down_w))
    da2 = links.scatter_plane(back_parts)
    output = (resid + links.scatter_plane(out_parts)).astype(bf16)

    dy = cotangent[0].astype(f32)
    sum_gain_ffn = jnp.sum(da2 * resid * r2, axis=0)
    dn2 = da2 * gain_f
    dresid = dy + r2 * (dn2 - resid * r2 * r2 * jnp.mean(dn2 * resid, axis=1, keepdims=True))
    dattn = jnp.concatenate(links.gather_plane(dresid.astype(bf16)))

    a2_all, dgu_all = jnp.concatenate(a2_chips), jnp.concatenate(dgus)
    hidden_all, dffn_all = jnp.concatenate(hiddens), jnp.concatenate(upstream_chips)
    grad_gate, grad_up = weights.ffn_in_back(dot(a2_all, dgu_all, 0, 0))
    grad_down = weights.ffn_out_back(dot(hidden_all, dffn_all, 0, 0))

    dnormed = dot(dattn, out_w, 1, 1).reshape(8, tokens, 2 * EP)
    dqkv, conv_tiles, mix_sums, group_sums = attend_back(
        mix, qkv, doc_col, doc_row, tt, group, dnormed, xhat, s, probs, zeroed
    )
    dqkv = dqkv.reshape(4, 2 * tokens, 6 * EP)
    da1 = links.scatter_plane([dot(dqkv[i], qkv_w, 1, 1) for i in range(4)])
    grad_out = weights.out_back(dot(normed.reshape(8 * tokens, 2 * EP), dattn, 0, 0))
    grad_qkv = weights.qkv_back(dot(a1, dqkv.reshape(8 * tokens, 6 * EP), 0, 0))

    r1 = rms_scale(xf)
    sum_gain_attn = jnp.sum(da1 * xf * r1, axis=0)
    dn1 = da1 * gain_a
    grad_x = dresid + r1 * (dn1 - xf * r1 * r1 * jnp.mean(dn1 * xf, axis=1, keepdims=True))

    place = lambda v: lax.dynamic_update_index_in_dim(jnp.zeros((8,) + v.shape, f32), v, weights.pair, 0)
    small = [
        sum_gain_attn,
        sum_gain_ffn,
        place(group_sums[0].reshape(2, EP)[:, :E].reshape(-1)),
        place(diagonals(conv_tiles)),
        place(jnp.sum(mix_sums[:4], axis=1)),
    ]
    sizes = [v.size for v in small]
    total = lax.psum(jnp.concatenate([v.reshape(-1) for v in small]), ("rep", "fsdp"))
    cut = [0]
    for size in sizes:
        cut.append(cut[-1] + size)
    gain_a_sum, gain_f_sum, group_sum, conv_sum, mix_sum = (total[cut[i] : cut[i + 1]] for i in range(5))
    rows = gain_attn.shape[0]
    own = lambda v: lax.dynamic_slice_in_dim(v, lax.axis_index("fsdp") * rows, rows, 0)
    return (
        output[None],
        grad_x[None],
        grad_qkv,
        grad_out,
        own(gain_a_sum),
        own(group_sum),
        conv_sum.reshape(H, QWIN, KWIN),
        mix_sum.reshape(H, 2),
        own(gain_f_sum),
        grad_gate,
        grad_up,
        grad_down,
    )


def join(bit, mine, other, axis):
    first, second = jnp.where(bit == 0, mine, other), jnp.where(bit == 0, other, mine)
    return jnp.stack([first, second], axis)


def fast(
    x_in,
    doc_ids,
    w_qkv,
    w_out,
    gain_attn,
    gain_group,
    conv_kernel,
    head_mix,
    gain_ffn,
    w_gate,
    w_up,
    w_down,
    cotangent,
):
    links = Links(16)
    pair = 4 * links.x + 2 * links.c + links.y
    tokens = x_in.shape[1]
    x, dy = x_in[0], cotangent[0]
    rows = w_qkv.shape[0]

    kernel = lax.dynamic_slice_in_dim(conv_kernel, 2 * pair, 2, 0)
    mix = lax.dynamic_slice_in_dim(head_mix, 2 * pair, 2, 0)
    gains = jnp.pad(jnp.stack([gain_attn, gain_group, gain_ffn]), ((0, 13), (0, 128 - rows)))
    docs = jnp.broadcast_to(doc_ids, (8, tokens))
    a1, dffn_1, docs, gains, qkv_w, gu_plane, out_w, th, tl, tt = start_call(
        x, dy, docs, gains, kernel.reshape(-1), w_qkv, w_gate, w_up, w_out, 1
    )
    docs = docs.reshape(8, 8, tokens)[:, 0]
    gain_a, gain_g, gain_f = gains[0:1], gains[1], gains[2:3]
    qkv_w = qkv_w.reshape(MODEL_WIDTH, 6 * EP)
    keep = lax.dynamic_index_in_dim(out_w, 2 * links.x + links.c, 0, keepdims=False)
    other = links.across("c", lax.dynamic_index_in_dim(out_w, 2 * links.x + 1 - links.c, 0, keepdims=False))
    out_w = jnp.pad(join(links.c, keep, other, 0), ((0, 0), (0, EP - E), (0, 0))).reshape(2 * EP, MODEL_WIDTH)

    group = lax.dynamic_slice_in_dim(gain_g.reshape(8, 2, E), pair, 1, 0)
    group = jnp.pad(group, ((0, 0), (0, 0), (0, EP - E))).reshape(1, 2 * EP)
    doc_col, doc_row = docs[:, :, None], docs[:, None, :]

    by_chip = lambda v: v.astype(bf16).reshape(4, 2, tokens, MODEL_WIDTH)
    by_row = lambda v: v.reshape(8, tokens, -1)
    qkv, normed, xhat, s, probs, zeroed, resid, a2, dffn_2, gu_w, down_w = forward_call(
        mix, by_row(a1), doc_col, doc_row, th, tl, group, qkv_w, out_w, x, dy, gain_f, gu_plane, w_down, 2
    )
    normed = normed.reshape(8 * tokens, 2 * EP)

    a2 = a2.reshape(8 * tokens, MODEL_WIDTH)
    flat = lambda v: v.reshape(-1, MODEL_WIDTH)
    gu_w = gu_w.reshape(MODEL_WIDTH, FF // 4)
    down_w = down_w.reshape(FF // 8, MODEL_WIDTH)
    dgu, hidden, grad_down = ffn_call(a2, flat(dffn_1), flat(dffn_2), gu_w, down_w)
    grad_down = grad_down.reshape(4, FF // 32, MODEL_WIDTH)
    dresid, dattn, sum_f, grad_down, grad_gate, grad_up, out_parts = mid_back_call(
        dgu, gu_w, a2, hidden, down_w, dy, resid, gain_f, grad_down, 3
    )

    grad_out = dot(normed, dattn.reshape(8 * tokens, MODEL_WIDTH), 0, 0).astype(bf16).reshape(2, EP, MODEL_WIDTH)[:, :rows]
    da_parts, grad_qkv, sum_a, conv_tiles, mix_sums, group_sums, out, grad_up, grad_out, grad_gate, grad_down = back_call(
        mix, qkv, doc_col, doc_row, tt, group, by_row(dattn), xhat, s, probs, zeroed, by_row(a1), out_w, qkv_w,
        out_parts, grad_up, grad_out, grad_gate, grad_down, resid, 5
    )
    sum_a = sum_a[0] / gain_a[0]
    place = lambda v: lax.dynamic_update_index_in_dim(jnp.zeros((8,) + v.shape, f32), v, pair, 0)
    small = [
        sum_a,
        sum_f[0],
        place(group_sums[0].reshape(2, EP)[:, :E].reshape(-1)),
        place(diagonals(conv_tiles)),
        place(jnp.sum(mix_sums[:4], axis=1)),
    ]
    cut = [0]
    for v in small:
        cut.append(cut[-1] + v.size)
    room = 48 * 128
    flat = jnp.concatenate([v.reshape(-1) for v in small] + [jnp.zeros((room - cut[-1],), f32)]).reshape(48, 128)
    grad_x, grad_qkv, grad_out, grad_up, total = end_call(
        by_chip(da_parts),
        grad_qkv.reshape(2, 4, 4 * rows, 3 * EP),
        grad_out,
        grad_up,
        flat,
        x,
        dresid,
        gain_a,
        4,
    )
    total = total.reshape(-1)
    gain_a_sum, gain_f_sum, group_sum, conv_sum, mix_sum = (total[cut[i] : cut[i + 1]] for i in range(5))
    own = lambda v: lax.dynamic_slice_in_dim(v, lax.axis_index("fsdp") * rows, rows, 0)
    return (
        out[None],
        grad_x[None],
        grad_qkv,
        grad_out,
        own(gain_a_sum),
        own(group_sum),
        conv_sum.reshape(H, QWIN, KWIN),
        mix_sum.reshape(H, 2),
        own(gain_f_sum),
        grad_gate,
        grad_up,
        grad_down,
    )


def solution(mesh):
    fsdp = mesh.shape["fsdp"]
    assert mesh.shape["rep"] == 2 and fsdp % 4 == 0
    rows, shard, part = P(("rep", "fsdp"), None, None), P("fsdp", None), P("fsdp")
    placed = (rows, P(("rep", "fsdp"), None), shard, shard, part, part, P(), P(), part, shard, shard, shard, rows)
    return jax.shard_map(
        fast if fsdp == 16 else (lambda *args: per_device(fsdp, *args)),
        mesh=mesh,
        in_specs=placed,
        out_specs=(rows, rows, shard, shard, part, part, P(), P(), part, shard, shard, shard),
        check_vma=False,
    )
```

profile of v0, /device:TPU:16, one launch (start us, length us, event | category | flops | bytes accessed | tf_op | source)
XLA Modules:
  0.0 461.4 jit_solution(1075078206396863010)
XLA Ops:
  0.6 0.0 copy-start
  0.7 0.7 copy-done
  1.4 0.1 constant_dynamic-slice_fusion.1
  1.5 0.1 copy.30
  1.7 0.7 reshape.187.taps_ref
  2.3 1.3 fusion.14.g_ref
  3.6 1.3 broadcast_in_dim.36.docs_ref
  4.9 72.1 %start.1 = (bf16[4,2,256,1536]{3,2,1,0:T(8,128)(2,1)}, bf16[4,2,128,1536]{3,2,1,0:T(8,128)(2,1)}, s32[4,2,8,256]{3,2,1,0:T(8,128)}, f32[8,1536]{1,0:T(8,128)}, b...) custom-call(bf16[256,1536]{1,0:T(8,128)(2,1)} %bitcast.75, ...), custom_call_target="tpu_custom_call" | custom-call | tf_op jit(solution)/shard_map/start/pallas_call | solution.py:536
  77.0 1.0 dynamic-slice_bitcast_fusion
  78.0 0.3 collective-permute-start
  78.3 0.0 copy-done.13
  78.3 0.1 constant_dynamic-slice_fusion.2
  78.4 0.7 copy.36.mix_ref
  79.1 1.4 fusion.15
  80.5 1.3 copy.31.dcol_ref
  81.8 1.5 fusion.17
  83.3 0.1 reshape_squeeze.6
  83.4 0.6 pad.13
  84.0 0.0 collective-permute-done
  84.0 1.0 fusion.3
  85.0 0.9 fusion.2
  85.9 88.2 %forward.1 = (bf16[8,256,768]{2,1,0:T(8,128)(2,1)}, bf16[8,256,256]{2,1,0:T(8,128)(2,1)}, f32[8,256,256]{2,1,0:T(8,128)}, f32[8,256,256]{2,1,0:T(8,128)}, f32[8,...) custom-call(f32[2,2]{1,0:T(2,128)} %copy.36.mix_ref, ...), custom_call_target="tpu_custom_call" | custom-call | tf_op jit(solution)/shard_map/forward/pallas_call | solution.py:832
  174.1 0.0 copy-done.3
  174.1 0.0 copy-start.2
  174.1 1.4 copy-done.2
  175.5 1.9 copy-done.4
  177.4 18.8 %ffn.1 = (bf16[2048,1024]{1,0:T(8,128)(2,1)}, bf16[2048,512]{1,0:T(8,128)(2,1)S(1)}, bf16[512,1536]{1,0:T(8,128)(2,1)S(1)}) custom-call(bf16[2048,1536]{1,0:T(8,128)(2,1)} %bitcast.62, bf16[1024,1536]{1,0:T(8,128)(2,1)S(1)} %bitcast.57, bf16[1024,1536]{1,0:T(8,128)(2,1)S(1)} %bitcast.58, bf16[1536,1024]{1,0:T(8,128)(2,1)} %bitcast.66, ...), custom_call_target="tpu_custom_call" | custom-call | tf_op jit(solution)/shard_map/ffn/pallas_call | solution.py:892
  196.2 1.3 copy-done.5
  197.5 1.1 copy-done.6
  198.7 90.3 %mid_back.1 = (f32[256,1536]{1,0:T(8,128)}, bf16[4,2,256,1536]{3,2,1,0:T(8,128)(2,1)}, f32[8,1536]{1,0:T(8,128)}, bf16[128,1536]{1,0:T(8,128)(2,1)}, bf16[384,51...) custom-call(bf16[2048,1024]{1,0:T(8,128)(2,1)} %get-tuple-element.74.dgu_ref, ...), custom_call_target="tpu_custom_call" | custom-call | tf_op jit(solution)/shard_map/mid_back/pallas_call | solution.py:536
  289.0 4.9 %convolution_convert_fusion = bf16[256,1536]{1,0:T(8,128)(2,1)S(1)} fusion(bf16[2048,256]{1,0:T(8,128)(2,1)} %bitcast.79, bf16[2048,1536]{1,0:T(8,128)(2,1)} %bitcast.60), kind=kOutput, calls=%fused_computation | convolution fusion | flops 1611005952 | bytes 8126464 | tf_op jit(solution)/shard_map/dot_general | solution.py:42
  293.9 0.9 slice.109.wo_ref
  294.8 70.0 %back.1 = (bf16[8,256,1536]{2,1,0:T(8,128)(2,1)}, bf16[2,1536,384]{2,1,0:T(8,128)(2,1)}, f32[8,1536]{1,0:T(8,128)}, f32[2,6,8,128]{3,2,1,0:T(8,128)}, f32[8,256]...) custom-call(f32[2,2]{1,0:T(2,128)} %copy.36.mix_ref, ...), custom_call_target="tpu_custom_call" | custom-call | tf_op jit(solution)/shard_map/back/pallas_call | solution.py:1356
  364.8 0.7 slice.88
  365.5 0.1 broadcast_in_dim.39
  365.6 0.1 reshape.205
  365.7 1.4 add_bitcast_fusion
  367.1 0.2 reshape.206
  367.3 0.8 slice_reduce_fusion.2
  368.1 0.1 reshape.207
  368.2 1.5 fusion.16
  369.7 0.7 concatenate.3
  370.3 72.1 %end.1 = (f32[256,1536]{1,0:T(8,128)}, f32[96,4608]{1,0:T(8,128)}, f32[96,1536]{1,0:T(8,128)}, f32[96,4096]{1,0:T(8,128)}, f32[48,128]{1,0:T(8,128)}) custom-call(bf16[4,2,256,1536]{3,2,1,0:T(8,128)(2,1)} %bitcast.78, bf16[2,4,384,384]{3,2,1,0:T(8,128)(2,1)} %bitcast.81, bf16[96,1536]{1,0:T(8,128)(2,1)} %get-tuple-element.91.wo_ref, ...), custom_call_target="tpu_custom_call" | custom-call | tf_op jit(solution)/shard_map/end/pallas_call | solution.py:536
  442.5 0.8 slice_bitcast_fusion
  443.3 2.4 slice.104
  445.7 0.6 dynamic_slice.30
  446.3 0.6 dynamic_slice.31
  446.9 0.7 slice.110
  447.6 0.2 reshape.210
  447.7 0.8 copy.34
  448.5 0.6 copy.35
  449.1 0.6 dynamic_slice.32
  449.7 2.1 copy.48
  451.8 0.0 copy-done.11
  451.8 1.1 copy.49
  452.9 0.9 copy-done.7
  453.8 1.2 copy.50
  455.0 0.2 copy-done.12
  455.2 0.8 copy.51
  456.1 1.1 copy.52
  457.2 0.8 copy-done.10
  458.0 1.1 copy.53
  459.2 0.8 copy-done.8
  460.0 1.1 copy.54
  (23 shorter events, 0.1 us)
Async XLA Ops:
  0.6 0.8 copy-start
  4.9 73.5 %copy-start.13 = (f32[16,2]{0,1:T(2,128)S(1)}, f32[16,2]{0,1:T(2,128)}, u32[]{:S(2)}) copy-start(f32[16,2]{0,1:T(2,128)} %param.20) | copy-start | bytes 388
  78.0 6.0 %collective-permute-start = (bf16[96,1536]{1,0:T(8,128)(2,1)S(1)}, bf16[96,1536]{1,0:T(8,128)(2,1)S(1)}, u32[]{:S(2)}, u32[]{:S(2)}) collective-permute-start(bf16[96,1536]{1,0:T(8,128)(2,1)S(1)} %dynamic-slice_bitcast_fusion), channel_id=1, source_target_pairs={{0,1},{1,0},{2,3},{3,2},{4,5},{5,4},{6,7},{7,6},{8,9},{9,8},{10,11... | collective-permute-start | bytes 884744 | tf_op jit(solution)/shard_map/ppermute | solution.py:1400
  85.9 88.2 %copy-start.3 = (bf16[4,2,128,1536]{3,2,1,0:T(8,128)(2,1)S(1)}, bf16[4,2,128,1536]{3,2,1,0:T(8,128)(2,1)}, u32[]{:S(2)}) copy-start(bf16[4,2,128,1536]{3,2,1,0:T(8,128)(2,1)} %get-tuple-element.70) | copy-start | bytes 9437188
  174.1 1.4 copy-start.2
  175.5 1.9 copy-start.4
  196.2 1.3 copy-start.5
  197.5 1.1 copy-start.6
  443.3 8.5 %copy-start.11 = (f32[256,1536]{1,0:T(8,128)S(1)}, f32[256,1536]{1,0:T(8,128)}, u32[]{:S(2)}) copy-start(f32[256,1536]{1,0:T(8,128)} %get-tuple-element.99) | copy-start | bytes 4718596
  451.8 2.0 copy-start.7
  453.8 1.4 copy-start.12
  453.8 2.3 copy-start.9
  456.1 2.0 copy-start.10
  458.0 2.0 copy-start.8
  458.0 3.1 copy-start.1
where the time goes:
time: 469 us; the launch traced here: 461 us
  Pallas kernels  412 us (88%)
  local copies, waits for them, and re-layouts  36.7 us (8%)
  other arithmetic  6.87 us (1%)
  matrix products  4.92 us (1%)
    pallas_call x3, Pallas kernels, comm_call(): pl.pallas_call(body, in_specs=in_specs, out_specs=out_specs, out_shape=ou...  235 us
    pallas_call x1, Pallas kernels, forward_call(): pl.pallas_call(body, grid=(rows,), in_specs=[pl.BlockSpec(memory_space=pl...  88.2 us
    pallas_call x1, Pallas kernels, back_call(): pl.pallas_call(body, grid=(rows,), in_specs=[pl.BlockSpec(memory_space=pl...  70 us
    unnamed x38, local copies, waits for them, and re-layouts  20 us
    pallas_call x1, Pallas kernels, ffn_call(): pl.pallas_call(body, grid=(4,), in_specs=[row(w), row(w, m // 2), row(w,...  18.8 us
  transfers between devices with their start and end apart: 1, of which 0 were waited for; matrix products, arithmetic and copies ran while one was open for 1% of the time, Pallas kernels for 0%

commit v1 on v0

--- a/solution.py
+++ b/solution.py
@@ -692,12 +692,16 @@
     )
 
 
-def forward_call(mix, a1, dcol, drow, th, tl, group, qkv_w, out_w, x, dy, gain, gu, w_down, ident):
+def turn(docs):
+    return jnp.transpose(docs)[:, 0:1], docs[0:1]
+
+
+def forward_call(mix, a1, docs, th, tl, group, qkv_w, out_w, x, dy, gain, gu, w_down, ident):
     rows, t, w = a1.shape
     n = x.shape[0]
     down = w_down.shape[0] // 2
 
-    def body(mix_ref, a1_ref, dcol_ref, drow_ref, th_ref, tl_ref, group_ref, qw_ref, ow_ref, x_ref, dy_ref, g_ref, gu_ref, wd_ref,
+    def body(mix_ref, a1_ref, docs_ref, th_ref, tl_ref, group_ref, qw_ref, ow_ref, x_ref, dy_ref, g_ref, gu_ref, wd_ref,
              qkv_ref, normed_ref, xhat_ref, s_ref, p_ref, z_ref, resid_ref, out_ref, dys_ref, gu_out, wd_out,
              parts, v, local, rc, rd, rx, ry, td, tx, ty, send, recv):
         net = Net()
@@ -732,7 +736,8 @@
             next(gather_dy)
 
         qkv_ref[0] = dot(a1_ref[0], qw_ref[...]).astype(bf16)
-        attend_row(mix_ref, qkv_ref, dcol_ref, drow_ref, th_ref, tl_ref, group_ref, normed_ref, xhat_ref, s_ref, p_ref, z_ref)
+        col, across = turn(docs_ref[0])
+        attend_row(mix_ref, qkv_ref, [col], [across], th_ref, tl_ref, group_ref, normed_ref, xhat_ref, s_ref, p_ref, z_ref)
         parts[3 - step // 2, step % 2] = dot(normed_ref[0], ow_ref[...]).astype(bf16)
 
         def swap(chip, i):
@@ -832,7 +837,7 @@
     return pl.pallas_call(
         body,
         grid=(rows,),
-        in_specs=[pl.BlockSpec(memory_space=pltpu.SMEM), row(t, w), row(t, 1), row(1, t), full(th), full(tl), full(group), full(qkv_w),
+        in_specs=[pl.BlockSpec(memory_space=pltpu.SMEM), row(t, w), row(8, t), full(th), full(tl), full(group), full(qkv_w),
                   full(out_w), full(x), full(dy), full(gain), full(gu), full(w_down)],
         out_specs=[row(t, 6 * EP), row(t, 2 * EP), row(t, 2 * EP), row(t, 2 * EP), row(2, t, t), row(2, t, t), keep(n, w), ANY, ANY, ANY, ANY],
         out_shape=[
@@ -852,7 +857,7 @@
         + dma_sems(SCATTER_COPIES + 2 * GATHER_COPIES + 2 * LINE_COPIES),
         compiler_params=pltpu.CompilerParams(collective_id=ident, has_side_effects=True, vmem_limit_bytes=60 << 20),
         name="forward",
-    )(mix, a1, dcol, drow, th, tl, group, qkv_w, out_w, x, dy, gain, gu, w_down)
+    )(mix, a1, docs, th, tl, group, qkv_w, out_w, x, dy, gain, gu, w_down)
 
 
 def ffn_call(a2, first, second, gu_w, down_w):
@@ -1106,7 +1111,7 @@
     rows, wide_q = qkv.shape[2] // 4, qkv.shape[3]
 
     def body(da_ref, q_ref, wo_ref, up_ref, small_ref, x_ref, dresid_ref, g_ref,
-             gx_ref, gq_ref, go_ref, gu_ref, total_ref,
+             gx_ref, gq_ref, go_ref, gu_ref, total_ref, own_ref,
              rc, rd, rx, ry, td, tx, ty, q_got, q_made, zq, cq, fq, cu, fu, ro, s_got, s_sum, s_line, send, recv):
         net = Net()
         sems = (send, recv)
@@ -1173,6 +1178,9 @@
         line_s.step(3)
         s_line[net.z] = s_sum[2]
         total_ref[...] = (s_line[0] + s_line[1]) + (s_line[2] + s_line[3])
+        own_ref[...] = jnp.zeros_like(own_ref)
+        for i in range(3):
+            own_ref[i : i + 1] = total_ref[pl.ds(16 * i + net.f, 1)]
         swap_o.wait_recv()
         go_ref[...] = wide(wo_ref[...]) + wide(ro[...])
         home_u.step(3)
@@ -1195,8 +1203,9 @@
     two = lambda specs: [pltpu.VMEM((2,) + v.shape, v.dtype) for v in specs]
     return comm_call(
         body, "end", ident, (da_parts, qkv, wo, gate_up, small, x, dresid, gain), [VM] * 8,
-        [shape((n, w), f32), shape((rows, 3 * MODEL_WIDTH), f32), shape(wo.shape, f32), shape((rows, FF), f32), shape(small.shape, f32)],
-        [VM] * 5,
+        [shape((n, w), f32), shape((rows, 3 * MODEL_WIDTH), f32), shape(wo.shape, f32), shape((rows, FF), f32), shape(small.shape, f32),
+         shape((8, small.shape[1]), f32)],
+        [VM] * 6,
         scatter_scratch(n, w) + two(line_scratch(4 * rows, wide_q)) + two([pltpu.VMEM((4 * rows, wide_q), bf16)])
         + two(home_scratch(rows, wide_q)) + home_scratch(rows, FF // 8) + [pltpu.VMEM(wo.shape, bf16)]
         + [pltpu.VMEM((3,) + small.shape, f32), pltpu.VMEM((3,) + small.shape, f32), pltpu.VMEM((4,) + small.shape, f32)]
@@ -1204,12 +1213,12 @@
     )
 
 
-def back_call(mix, qkv, dcol, drow, tt, gain, dattn, xhat, s, p, z, a1, out_w, qkv_w, out_parts, up_parts, wo, gate, down, resid, ident):
+def back_call(mix, qkv, docs, tt, gain, dattn, xhat, s, p, z, a1, out_w, qkv_w, out_parts, up_parts, wo, gate, down, resid, ident):
     rows, t, _ = qkv.shape
     n, w = out_parts.shape[2:]
     rows_o, rows_d, wide_q = wo.shape[1], down.shape[0], 3 * EP
 
-    def body(mix_ref, qkv_ref, dcol_ref, drow_ref, tt_ref, gain_ref, dattn_ref, xhat_ref, s_ref, p_ref, z_ref, a1_ref,
+    def body(mix_ref, qkv_ref, docs_ref, tt_ref, gain_ref, dattn_ref, xhat_ref, s_ref, p_ref, z_ref, a1_ref,
              ow_ref, qw_ref, op_ref, gu_ref, wo_ref, gate_ref, down_ref, resid_ref,
              da_ref, q16_ref, sum_ref, gconv_ref, gmix_ref, gg_ref, out_ref, gu_out, go_out, gg_out, gd_ref,
              m_ref, gq_ref, dq, rc, rd, rx, ry, td, tx, ty, g_got, g_made, o_got, o_made, po, cg, fg, fd, send, recv):
@@ -1241,7 +1250,7 @@
             gg_ref[...] = jnp.zeros_like(gg_ref)
             gq_ref[...] = jnp.zeros_like(gq_ref)
 
-        allowed = allowed_mask(dcol_ref[0], drow_ref[0])
+        allowed = allowed_mask(*turn(docs_ref[0]))
         scale = 1.0 / math.sqrt(E)
         lane = lax.broadcasted_iota(jnp.int32, (1, EP), 1)
         prob = [p_ref[0, 0], p_ref[0, 1]]
@@ -1356,7 +1365,7 @@
     return pl.pallas_call(
         body,
         grid=(rows,),
-        in_specs=[pl.BlockSpec(memory_space=pltpu.SMEM), row(t, 6 * EP), row(t, 1), row(1, t), full(tt), full(gain),
+        in_specs=[pl.BlockSpec(memory_space=pltpu.SMEM), row(t, 6 * EP), row(8, t), full(tt), full(gain),
                   row(t, w), row(t, 2 * EP), row(t, 2 * EP), row(2, t, t), row(2, t, t), row(t, w),
                   full(out_w), full(qkv_w), full(out_parts), full(up_parts), full(wo), full(gate), full(down), full(resid)],
         out_specs=[row(t, w), keep(2, w, wide_q), keep(8, w), keep(2, QWIN, 8, EP), keep(8, t), keep(8, 2 * EP), keep(n, w),
@@ -1379,7 +1388,7 @@
         + home_scratch(rows_o, FF // 8) + [pltpu.VMEM((2, rows_d, w), bf16)] + dma_sems(SCATTER_COPIES + 18),
         compiler_params=pltpu.CompilerParams(collective_id=ident, has_side_effects=True, vmem_limit_bytes=63 << 20),
         name="back",
-    )(mix, qkv, dcol, drow, tt, gain, dattn, xhat, s, p, z, a1, out_w, qkv_w, out_parts, up_parts, wo, gate, down, resid)
+    )(mix, qkv, docs, tt, gain, dattn, xhat, s, p, z, a1, out_w, qkv_w, out_parts, up_parts, wo, gate, down, resid)
 
 
 def rms_scale(values):
@@ -1737,7 +1746,7 @@
     a1, dffn_1, docs, gains, qkv_w, gu_plane, out_w, th, tl, tt = start_call(
         x, dy, docs, gains, kernel.reshape(-1), w_qkv, w_gate, w_up, w_out, 1
     )
-    docs = docs.reshape(8, 8, tokens)[:, 0]
+    docs = docs.reshape(8, 8, tokens)
     gain_a, gain_g, gain_f = gains[0:1], gains[1], gains[2:3]
     qkv_w = qkv_w.reshape(MODEL_WIDTH, 6 * EP)
     keep = lax.dynamic_index_in_dim(out_w, 2 * links.x + links.c, 0, keepdims=False)
@@ -1746,12 +1755,11 @@
 
     group = lax.dynamic_slice_in_dim(gain_g.reshape(8, 2, E), pair, 1, 0)
     group = jnp.pad(group, ((0, 0), (0, 0), (0, EP - E))).reshape(1, 2 * EP)
-    doc_col, doc_row = docs[:, :, None], docs[:, None, :]
 
     by_chip = lambda v: v.astype(bf16).reshape(4, 2, tokens, MODEL_WIDTH)
     by_row = lambda v: v.reshape(8, tokens, -1)
     qkv, normed, xhat, s, probs, zeroed, resid, a2, dffn_2, gu_w, down_w = forward_call(
-        mix, by_row(a1), doc_col, doc_row, th, tl, group, qkv_w, out_w, x, dy, gain_f, gu_plane, w_down, 2
+        mix, by_row(a1), docs, th, tl, group, qkv_w, out_w, x, dy, gain_f, gu_plane, w_down, 2
     )
     normed = normed.reshape(8 * tokens, 2 * EP)
 
@@ -1767,47 +1775,37 @@
 
     grad_out = dot(normed, dattn.reshape(8 * tokens, MODEL_WIDTH), 0, 0).astype(bf16).reshape(2, EP, MODEL_WIDTH)[:, :rows]
     da_parts, grad_qkv, sum_a, conv_tiles, mix_sums, group_sums, out, grad_up, grad_out, grad_gate, grad_down = back_call(
-        mix, qkv, doc_col, doc_row, tt, group, by_row(dattn), xhat, s, probs, zeroed, by_row(a1), out_w, qkv_w,
+        mix, qkv, docs, tt, group, by_row(dattn), xhat, s, probs, zeroed, by_row(a1), out_w, qkv_w,
         out_parts, grad_up, grad_out, grad_gate, grad_down, resid, 5
     )
     sum_a = sum_a[0] / gain_a[0]
-    place = lambda v: lax.dynamic_update_index_in_dim(jnp.zeros((8,) + v.shape, f32), v, pair, 0)
-    small = [
-        sum_a,
-        sum_f[0],
-        place(group_sums[0].reshape(2, EP)[:, :E].reshape(-1)),
-        place(diagonals(conv_tiles)),
-        place(jnp.sum(mix_sums[:4], axis=1)),
-    ]
-    cut = [0]
-    for v in small:
-        cut.append(cut[-1] + v.size)
-    room = 48 * 128
-    flat = jnp.concatenate([v.reshape(-1) for v in small] + [jnp.zeros((room - cut[-1],), f32)]).reshape(48, 128)
-    grad_x, grad_qkv, grad_out, grad_up, total = end_call(
+    place = lambda v: lax.dynamic_update_index_in_dim(jnp.zeros((8,) + v.shape, f32), v, pair, 0).reshape(16, -1)
+    heads = jnp.concatenate([diagonals(conv_tiles).reshape(2, -1), jnp.sum(mix_sums[:4], axis=1).reshape(2, 2)], 1)
+    small = [sum_a.reshape(16, -1), sum_f[0].reshape(16, -1), place(group_sums[0].reshape(2, EP)[:, :E]), place(heads)]
+    small = jnp.concatenate([jnp.pad(v, ((0, 0), (0, 128 - v.shape[1]))) for v in small])
+    grad_x, grad_qkv, grad_out, grad_up, total, own = end_call(
         by_chip(da_parts),
         grad_qkv.reshape(2, 4, 4 * rows, 3 * EP),
         grad_out,
         grad_up,
-        flat,
+        small,
         x,
         dresid,
         gain_a,
         4,
     )
-    total = total.reshape(-1)
-    gain_a_sum, gain_f_sum, group_sum, conv_sum, mix_sum = (total[cut[i] : cut[i + 1]] for i in range(5))
-    own = lambda v: lax.dynamic_slice_in_dim(v, lax.axis_index("fsdp") * rows, rows, 0)
+    heads = total[48:]
+    taps = QWIN * KWIN
     return (
         out[None],
         grad_x[None],
         grad_qkv,
         grad_out,
-        own(gain_a_sum),
-        own(group_sum),
-        conv_sum.reshape(H, QWIN, KWIN),
-        mix_sum.reshape(H, 2),
-        own(gain_f_sum),
+        own[0, :rows],
+        own[2, :rows],
+        heads[:, :taps].reshape(H, QWIN, KWIN),
+        heads[:, taps : taps + 2],
+        own[1, :rows],
         grad_gate,
         grad_up,
         grad_down,

time: 469 us -> 463 us (0.987)
  local copies, waits for them, and re-layouts: 36.7 us -> 29.8 us
    unnamed x38 -> x40, local copies, waits for them, and re-layouts: 20 us -> 18.8 us
where the time goes in v1:
time: 463 us; the launch traced here: 457 us
  Pallas kernels  413 us (89%)
  local copies, waits for them, and re-layouts  29.8 us (6%)
  other arithmetic  7.57 us (2%)
  matrix products  4.92 us (1%)
    pallas_call x3, Pallas kernels, comm_call(): pl.pallas_call(body, in_specs=in_specs, out_specs=out_specs, out_shape=ou...  236 us
    pallas_call x1, Pallas kernels, forward_call(): pl.pallas_call(body, grid=(rows,), in_specs=[pl.BlockSpec(memory_space=pl...  88.1 us
    pallas_call x1, Pallas kernels, back_call(): pl.pallas_call(body, grid=(rows,), in_specs=[pl.BlockSpec(memory_space=pl...  69.8 us
    unnamed x40, local copies, waits for them, and re-layouts  18.8 us
    pallas_call x1, Pallas kernels, ffn_call(): pl.pallas_call(body, grid=(4,), in_specs=[row(w), row(w, m // 2), row(w,...  18.8 us
  transfers between devices with their start and end apart: 1, of which 0 were waited for; matrix products, arithmetic and copies ran while one was open for 1% of the time, Pallas kernels for 0%

profile of v1, /device:TPU:16, one launch (start us, length us, event | category | flops | bytes accessed | tf_op | source)
XLA Modules:
  0.0 456.6 jit_solution(11368742600529253227)
XLA Ops:
  0.6 0.0 copy-start
  0.7 0.7 copy-done
  1.4 0.1 constant_dynamic-slice_fusion.1
  1.5 0.1 copy.29
  1.7 0.7 reshape.108.taps_ref
  2.3 1.3 fusion.16.g_ref
  3.6 1.3 broadcast_in_dim.28.docs_ref
  4.9 72.1 %start.1 = (bf16[4,2,256,1536]{3,2,1,0:T(8,128)(2,1)}, bf16[4,2,128,1536]{3,2,1,0:T(8,128)(2,1)}, s32[4,2,8,256]{3,2,1,0:T(8,128)}, f32[8,1536]{1,0:T(8,128)}, b...) custom-call(bf16[256,1536]{1,0:T(8,128)(2,1)} %bitcast.73, ...), custom_call_target="tpu_custom_call" | custom-call | tf_op jit(solution)/shard_map/start/pallas_call | solution.py:536
  77.0 1.0 dynamic-slice_bitcast_fusion
  78.0 0.3 collective-permute-start
  78.3 0.0 copy-done.14
  78.3 0.1 constant_dynamic-slice_fusion.2
  78.4 0.7 copy.32.mix_ref
  79.0 1.5 fusion.18
  80.5 0.1 reshape_squeeze.9
  80.6 0.6 pad.27
  81.2 0.0 collective-permute-done
  81.2 1.0 fusion.3
  82.2 0.9 fusion.2
  83.1 88.1 %forward.1 = (bf16[8,256,768]{2,1,0:T(8,128)(2,1)}, bf16[8,256,256]{2,1,0:T(8,128)(2,1)}, f32[8,256,256]{2,1,0:T(8,128)}, f32[8,256,256]{2,1,0:T(8,128)}, f32[8,...) custom-call(f32[2,2]{1,0:T(2,128)} %copy.32.mix_ref, ...), custom_call_target="tpu_custom_call" | custom-call | tf_op jit(solution)/shard_map/forward/pallas_call | solution.py:837
  171.2 0.0 copy-done.3
  171.2 0.0 copy-start.2
  171.2 1.4 copy-done.2
  172.6 1.9 copy-done.4
  174.5 18.8 %ffn.1 = (bf16[2048,1024]{1,0:T(8,128)(2,1)}, bf16[2048,512]{1,0:T(8,128)(2,1)S(1)}, bf16[512,1536]{1,0:T(8,128)(2,1)S(1)}) custom-call(bf16[2048,1536]{1,0:T(8,128)(2,1)} %bitcast.62, bf16[1024,1536]{1,0:T(8,128)(2,1)S(1)} %bitcast.57, bf16[1024,1536]{1,0:T(8,128)(2,1)S(1)} %bitcast.58, bf16[1536,1024]{1,0:T(8,128)(2,1)} %bitcast.66, ...), custom_call_target="tpu_custom_call" | custom-call | tf_op jit(solution)/shard_map/ffn/pallas_call | solution.py:897
  193.3 1.3 copy-done.5
  194.7 1.1 copy-done.6
  195.8 91.4 %mid_back.1 = (f32[256,1536]{1,0:T(8,128)}, bf16[4,2,256,1536]{3,2,1,0:T(8,128)(2,1)}, f32[8,1536]{1,0:T(8,128)}, bf16[128,1536]{1,0:T(8,128)(2,1)}, bf16[384,51...) custom-call(bf16[2048,1024]{1,0:T(8,128)(2,1)} %get-tuple-element.75.dgu_ref, ...), custom_call_target="tpu_custom_call" | custom-call | tf_op jit(solution)/shard_map/mid_back/pallas_call | solution.py:536
  287.2 4.9 %convolution_convert_fusion = bf16[256,1536]{1,0:T(8,128)(2,1)S(1)} fusion(bf16[2048,256]{1,0:T(8,128)(2,1)} %bitcast.79, bf16[2048,1536]{1,0:T(8,128)(2,1)} %bitcast.60), kind=kOutput, calls=%fused_computation | convolution fusion | flops 1611005952 | bytes 8126464 | tf_op jit(solution)/shard_map/dot_general | solution.py:42
  292.1 0.9 slice.91.wo_ref
  293.0 69.8 %back.1 = (bf16[8,256,1536]{2,1,0:T(8,128)(2,1)}, bf16[2,1536,384]{2,1,0:T(8,128)(2,1)}, f32[8,1536]{1,0:T(8,128)}, f32[2,6,8,128]{3,2,1,0:T(8,128)}, f32[8,256]...) custom-call(f32[2,2]{1,0:T(2,128)} %copy.32.mix_ref, ...), custom_call_target="tpu_custom_call" | custom-call | tf_op jit(solution)/shard_map/back/pallas_call | solution.py:1365
  362.8 0.8 slice_reduce_fusion.2
  363.6 0.1 reshape.127
  363.7 1.4 add_reduce_fusion
  365.1 0.1 reshape.132
  365.2 0.7 slice.75
  365.9 0.8 slice_reduce_fusion
  366.7 0.1 reshape_squeeze.10
  366.8 1.4 fusion.17
  368.2 0.1 div.19
  368.3 0.1 constant_dynamic-update-slice_fusion
  368.4 0.6 select_maximum_fusion.small_ref
  369.0 72.8 %end.1 = (f32[256,1536]{1,0:T(8,128)}, f32[96,4608]{1,0:T(8,128)}, f32[96,1536]{1,0:T(8,128)}, f32[96,4096]{1,0:T(8,128)}, f32[64,128]{1,0:T(8,128)}, /*index=5*/f32[8,128]{1,0:T(8,128)}) custom-call(bf16[4,2,256,1536]{3,2,1,0:T(8,128)(2,1)} %bitcast.78, bf16[2,4,384,384]{3,2,1,0:T(8,128)(2,1)} %bitcast.81, bf16[96,1536]{1,0:T(8,128)(2,1)} %get-tuple-element.92.wo_ref, ...), custom_call_target="tpu_custom_call" | custom-call | tf_op jit(solution)/shard_map/end/pallas_call | solution.py:536
  441.8 0.0 copy-start.11
  441.8 0.8 slice.88
  442.6 0.8 slice.89
  443.4 1.3 slice_bitcast_fusion
  444.7 0.1 reshape.129
  444.8 0.8 copy.30
  445.5 0.6 copy.31
  446.2 0.9 copy.42
  447.1 0.0 copy-done.11
  447.1 1.1 copy.43
  448.2 0.9 copy-done.7
  449.1 1.2 copy.44
  450.3 0.2 copy-done.13
  450.5 0.8 copy.45
  451.4 0.0 copy-done.9
  451.4 1.1 copy.46
  452.5 0.8 copy-done.10
  453.3 1.1 copy.47
  454.5 0.8 copy-done.8
  455.3 1.1 copy.48
  456.5 0.0 copy-done.1
  (17 shorter events, 0.0 us)
Async XLA Ops:
  0.6 0.8 copy-start
  4.9 73.4 %copy-start.14 = (f32[16,2]{0,1:T(2,128)S(1)}, f32[16,2]{0,1:T(2,128)}, u32[]{:S(2)}) copy-start(f32[16,2]{0,1:T(2,128)} %param.20) | copy-start | bytes 388
  78.0 3.2 collective-permute-start
  83.1 88.1 %copy-start.3 = (bf16[4,2,128,1536]{3,2,1,0:T(8,128)(2,1)S(1)}, bf16[4,2,128,1536]{3,2,1,0:T(8,128)(2,1)}, u32[]{:S(2)}) copy-start(bf16[4,2,128,1536]{3,2,1,0:T(8,128)(2,1)} %get-tuple-element.71) | copy-start | bytes 9437188
  171.2 1.4 copy-start.2
  172.6 1.9 copy-start.4
  193.3 1.3 copy-start.5
  194.6 1.1 copy-start.6
  369.0 77.2 %copy-start.12 = (bf16[256,1536]{1,0:T(8,128)(2,1)S(1)}, bf16[256,1536]{1,0:T(8,128)(2,1)}, u32[]{:S(2)}) copy-start(bf16[256,1536]{1,0:T(8,128)(2,1)} %get-tuple-element.89) | copy-start | bytes 2359300
  441.8 5.3 %copy-start.11 = (f32[256,1536]{1,0:T(8,128)S(1)}, f32[256,1536]{1,0:T(8,128)}, u32[]{:S(2)}) copy-start(f32[256,1536]{1,0:T(8,128)} %get-tuple-element.100) | copy-start | bytes 4718596
  447.1 2.0 copy-start.7
  449.1 1.4 copy-start.13
  449.1 2.3 copy-start.9
  451.4 2.0 copy-start.10
  453.3 2.0 copy-start.8
  453.3 3.1 copy-start.1

commit v2 on v1

--- a/solution.py
+++ b/solution.py
@@ -901,7 +901,7 @@
         out_specs=[row(2 * half), row(half), pl.BlockSpec((half, w), lambda i: (0, 0))],
         out_shape=[shape((count, 2 * half), bf16), shape((count, half), bf16), shape((half, w), bf16)],
         scratch_shapes=[pltpu.VMEM((m, w), bf16), pltpu.VMEM((half, w), f32)],
-        compiler_params=pltpu.CompilerParams(vmem_limit_bytes=40 << 20),
+        compiler_params=pltpu.CompilerParams(vmem_limit_bytes=63 << 20),
         name="ffn",
     )(a2, first, second, gu_w, down_w)
 

time: 463 us -> 459 us (level)
  local copies, waits for them, and re-layouts: 29.8 us -> 24.1 us
    unnamed x40 -> x30, local copies, waits for them, and re-layouts: 18.8 us -> 13.1 us
where the time goes in v2:
time: 459 us; the launch traced here: 452 us
  Pallas kernels  414 us (90%)
  local copies, waits for them, and re-layouts  24.1 us (5%)
  other arithmetic  7.56 us (2%)
  matrix products  4.92 us (1%)
    pallas_call x3, Pallas kernels, comm_call(): pl.pallas_call(body, in_specs=in_specs, out_specs=out_specs, out_shape=ou...  236 us
    pallas_call x1, Pallas kernels, forward_call(): pl.pallas_call(body, grid=(rows,), in_specs=[pl.BlockSpec(memory_space=pl...  88 us
    pallas_call x1, Pallas kernels, back_call(): pl.pallas_call(body, grid=(rows,), in_specs=[pl.BlockSpec(memory_space=pl...  69.8 us
    pallas_call x1, Pallas kernels, ffn_call(): pl.pallas_call(body, grid=(4,), in_specs=[row(w), row(w, m // 2), row(w,...  20.1 us
    unnamed x30, local copies, waits for them, and re-layouts  13.1 us
  transfers between devices with their start and end apart: 1, of which 0 were waited for; matrix products, arithmetic and copies ran while one was open for 1% of the time, Pallas kernels for 0%

profile of v2, /device:TPU:16, one launch (start us, length us, event | category | flops | bytes accessed | tf_op | source)
XLA Modules:
  0.0 452.2 jit_solution(17799662377623026800)
XLA Ops:
  0.6 0.0 copy-start
  0.7 0.7 copy-done
  1.4 0.1 constant_dynamic-slice_fusion.1
  1.5 0.1 copy.29
  1.7 0.7 reshape.108.taps_ref
  2.3 1.3 fusion.16.g_ref
  3.6 1.3 broadcast_in_dim.28.docs_ref
  4.9 0.0 copy-start.9
  4.9 72.1 %start.1 = (bf16[4,2,256,1536]{3,2,1,0:T(8,128)(2,1)}, bf16[4,2,128,1536]{3,2,1,0:T(8,128)(2,1)}, s32[4,2,8,256]{3,2,1,0:T(8,128)}, f32[8,1536]{1,0:T(8,128)}, b...) custom-call(bf16[256,1536]{1,0:T(8,128)(2,1)} %bitcast.68, ...), custom_call_target="tpu_custom_call" | custom-call | tf_op jit(solution)/shard_map/start/pallas_call | solution.py:536
  77.0 1.0 dynamic-slice_bitcast_fusion
  78.0 0.3 collective-permute-start
  78.3 0.0 copy-done.9
  78.3 0.1 constant_dynamic-slice_fusion.2
  78.4 0.7 copy.32.mix_ref
  79.0 1.5 fusion.18
  80.5 0.1 reshape_squeeze.9
  80.6 0.6 pad.27
  81.2 0.0 collective-permute-done
  81.2 1.0 fusion.3
  82.2 0.9 fusion.2
  83.1 88.0 %forward.1 = (bf16[8,256,768]{2,1,0:T(8,128)(2,1)}, bf16[8,256,256]{2,1,0:T(8,128)(2,1)}, f32[8,256,256]{2,1,0:T(8,128)}, f32[8,256,256]{2,1,0:T(8,128)}, f32[8,...) custom-call(f32[2,2]{1,0:T(2,128)} %copy.32.mix_ref, ...), custom_call_target="tpu_custom_call" | custom-call | tf_op jit(solution)/shard_map/forward/pallas_call | solution.py:837
  171.1 20.1 %ffn.1 = (bf16[2048,1024]{1,0:T(8,128)(2,1)}, bf16[2048,512]{1,0:T(8,128)(2,1)}, bf16[512,1536]{1,0:T(8,128)(2,1)}) custom-call(bf16[2048,1536]{1,0:T(8,128)(2,1)} %bitcast.57, bf16[1024,1536]{1,0:T(8,128)(2,1)} %bitcast.77, bf16[1024,1536]{1,0:T(8,128)(2,1)} %bitcast.78, bf16[1536,1024]{1,0:T(8,128)(2,1)} %bitcast.61, bf16[512,1536]{1,0:T(8,128)(2,1)} %bitcast.73), custom_call_target="tpu_custom_call" | custom-call | tf_op jit(solution)/shard_map/ffn/pallas_call | solution.py:897
  191.2 91.5 %mid_back.1 = (f32[256,1536]{1,0:T(8,128)}, bf16[4,2,256,1536]{3,2,1,0:T(8,128)(2,1)}, f32[8,1536]{1,0:T(8,128)}, bf16[128,1536]{1,0:T(8,128)(2,1)}, bf16[384,51...) custom-call(bf16[2048,1024]{1,0:T(8,128)(2,1)} %get-tuple-element.75.dgu_ref, ...), custom_call_target="tpu_custom_call" | custom-call | tf_op jit(solution)/shard_map/mid_back/pallas_call | solution.py:536
  282.7 4.9 %convolution_convert_fusion = bf16[256,1536]{1,0:T(8,128)(2,1)S(1)} fusion(bf16[2048,256]{1,0:T(8,128)(2,1)} %bitcast.76, bf16[2048,1536]{1,0:T(8,128)(2,1)} %bitcast.55), kind=kOutput, calls=%fused_computation | convolution fusion | flops 1611005952 | bytes 8126464 | tf_op jit(solution)/shard_map/dot_general | solution.py:42
  287.6 0.9 slice.91.wo_ref
  288.5 69.8 %back.1 = (bf16[8,256,1536]{2,1,0:T(8,128)(2,1)}, bf16[2,1536,384]{2,1,0:T(8,128)(2,1)}, f32[8,1536]{1,0:T(8,128)}, f32[2,6,8,128]{3,2,1,0:T(8,128)}, f32[8,256]...) custom-call(f32[2,2]{1,0:T(2,128)} %copy.32.mix_ref, ...), custom_call_target="tpu_custom_call" | custom-call | tf_op jit(solution)/shard_map/back/pallas_call | solution.py:1365
  358.3 0.8 slice_reduce_fusion.2
  359.1 0.1 reshape.127
  359.2 1.4 add_reduce_fusion
  360.6 0.1 reshape.132
  360.7 0.7 slice.75
  361.4 0.8 slice_reduce_fusion
  362.2 0.1 reshape_squeeze.10
  362.3 1.4 fusion.17
  363.7 0.1 div.19
  363.8 0.1 constant_dynamic-update-slice_fusion
  363.9 0.6 select_maximum_fusion.small_ref
  364.5 0.0 copy-start.7
  364.5 72.8 %end.1 = (f32[256,1536]{1,0:T(8,128)}, f32[96,4608]{1,0:T(8,128)}, f32[96,1536]{1,0:T(8,128)}, f32[96,4096]{1,0:T(8,128)}, f32[64,128]{1,0:T(8,128)}, /*index=5*/f32[8,128]{1,0:T(8,128)}) custom-call(bf16[4,2,256,1536]{3,2,1,0:T(8,128)(2,1)} %bitcast.75, bf16[2,4,384,384]{3,2,1,0:T(8,128)(2,1)} %bitcast.80, bf16[96,1536]{1,0:T(8,128)(2,1)} %get-tuple-element.92.wo_ref, ...), custom_call_target="tpu_custom_call" | custom-call | tf_op jit(solution)/shard_map/end/pallas_call | solution.py:536
  437.3 0.0 copy-start.6
  437.3 0.8 slice.88
  438.1 0.8 slice.89
  438.9 1.3 slice_bitcast_fusion
  440.2 0.1 reshape.129
  440.3 0.8 copy.30
  441.0 0.6 copy.31
  441.7 0.0 copy-done.7
  441.7 0.9 copy.42
  442.6 0.0 copy-done.6
  442.6 0.0 copy-start.2
  442.6 1.1 copy.43
  443.7 0.9 copy-done.2
  444.6 0.0 copy-start.8
  444.6 0.0 copy-start.4
  444.6 1.2 copy.44
  445.8 0.2 copy-done.8
  446.1 0.8 copy.45
  446.9 0.0 copy-done.4
  446.9 1.1 copy.46
  448.0 0.8 copy-done.5
  448.9 1.1 copy.47
  450.0 0.8 copy-done.3
  450.8 1.1 copy.48
  452.0 0.0 copy-done.1
  (7 shorter events, 0.0 us)
Async XLA Ops:
  0.6 0.8 copy-start
  4.9 73.4 %copy-start.9 = (f32[16,2]{0,1:T(2,128)S(1)}, f32[16,2]{0,1:T(2,128)}, u32[]{:S(2)}) copy-start(f32[16,2]{0,1:T(2,128)} %param.20) | copy-start | bytes 388
  78.0 3.2 collective-permute-start
  364.5 77.2 %copy-start.7 = (bf16[256,1536]{1,0:T(8,128)(2,1)S(1)}, bf16[256,1536]{1,0:T(8,128)(2,1)}, u32[]{:S(2)}) copy-start(bf16[256,1536]{1,0:T(8,128)(2,1)} %get-tuple-element.89) | copy-start | bytes 2359300
  437.3 5.3 %copy-start.6 = (f32[256,1536]{1,0:T(8,128)S(1)}, f32[256,1536]{1,0:T(8,128)}, u32[]{:S(2)}) copy-start(f32[256,1536]{1,0:T(8,128)} %get-tuple-element.100) | copy-start | bytes 4718596
  442.6 2.0 copy-start.2
  444.6 1.4 copy-start.8
  444.6 2.3 copy-start.4
  446.9 2.0 copy-start.5
  448.9 2.0 copy-start.3
  448.9 3.1 copy-start.1
